TPU v7x, 8 devices: a whole 2x2x1 slice. The times are simulated.
8 devices in a mesh: dp: 1 (over z), ep: 8 (over y, x, core).
Axes of the slice: x: 2, y: 2, z: 1, core: 2. Of those that a mesh axis runs over, the one named last changes fastest.
Arguments:
- tokens_a: bfloat16 [256, 1536], P(('dp', 'ep'))
- experts_a: int32 [256, 8], P(('dp', 'ep'))
- slots_a: int32 [256, 8], P(('dp', 'ep'))
- gates_a: bfloat16 [256, 8], P(('dp', 'ep'))
- tokens_b: bfloat16 [256, 1536], P(('dp', 'ep'))
- experts_b: int32 [256, 8], P(('dp', 'ep'))
- slots_b: int32 [256, 8], P(('dp', 'ep'))
- gates_b: bfloat16 [256, 8], P(('dp', 'ep'))
- attn_gain: bfloat16 [1536], replicated
- w_query: bfloat16 [1536, 24, 64], replicated
- w_key: bfloat16 [1536, 24, 64], replicated
- w_value: bfloat16 [1536, 24, 64], replicated
- w_out: bfloat16 [24, 64, 1536], replicated
- moe_gain: bfloat16 [1536], replicated
- w_gate: bfloat16 [40, 1536, 512], P('ep')
- w_up: bfloat16 [40, 1536, 512], P('ep')
- w_down: bfloat16 [40, 512, 1536], P('ep')
Outputs:
- output 1: bfloat16 [256, 1536], P(('dp', 'ep'))
- output 2: bfloat16 [256, 1536], P(('dp', 'ep'))
All inputs are finite; a program needn't handle non-finite values.
Results may differ from a plain program's by a relative error of at most 0.0137999.
Values are sent between devices in bfloat16 or wider.
A program may use at most 1 GiB of HBM per device.

v0:
```python
import jax
import jax.numpy as jnp
from jax import lax
from jax.sharding import PartitionSpec as P

NORM_EPS = 1e-6
MASK_VALUE = -1e30


def rms_norm(rows, gain_vec):
    rows_f = rows.astype(jnp.float32)
    inv_rms = lax.rsqrt(jnp.mean(rows_f * rows_f, axis=-1, keepdims=True) + NORM_EPS)
    return (rows_f * inv_rms * gain_vec.astype(jnp.float32)).astype(jnp.bfloat16)


def attention_block(sequence, attn_gain, w_query, w_key, w_value, w_out):
    seq_len = sequence.shape[0]
    normed = rms_norm(sequence, attn_gain)
    query = jnp.einsum("td,dhe->the", normed, w_query, preferred_element_type=jnp.float32).astype(jnp.bfloat16)
    keys = jnp.einsum("td,dhe->the", normed, w_key, preferred_element_type=jnp.float32).astype(jnp.bfloat16)
    values = jnp.einsum("td,dhe->the", normed, w_value, preferred_element_type=jnp.float32).astype(jnp.bfloat16)
    scores = jnp.einsum("qhe,khe->hqk", query, keys, preferred_element_type=jnp.float32) * (w_query.shape[2] ** -0.5)
    causal = lax.broadcasted_iota(jnp.int32, (seq_len, seq_len), 0) >= lax.broadcasted_iota(jnp.int32, (seq_len, seq_len), 1)
    scores = jnp.where(causal[None, :, :], scores, MASK_VALUE)
    attn_prob = jax.nn.softmax(scores, axis=-1).astype(jnp.bfloat16)
    context = jnp.einsum("hqk,khe->qhe", attn_prob, values, preferred_element_type=jnp.float32).astype(jnp.bfloat16)
    attn_out = jnp.einsum("qhe,hed->qd", context, w_out, preferred_element_type=jnp.float32)
    return (sequence.astype(jnp.float32) + attn_out).astype(jnp.bfloat16)


def capacity_of(seq_len, top_k, experts_total):
    return 8 * max(1, (seq_len * top_k) // (4 * experts_total))


def dispatch_rows(normed, dest_row, experts_total, capacity):
    seq_len, model_dim = normed.shape
    top_k = dest_row.shape[0] // seq_len
    token_of = jnp.arange(seq_len * top_k, dtype=jnp.int32) // top_k
    source = jnp.full((experts_total * capacity,), seq_len, jnp.int32).at[dest_row].set(token_of, mode="drop")
    return jnp.take(normed, source, axis=0, mode="fill", fill_value=0).reshape(experts_total, capacity, model_dim)


def combine_rows(residual, returned, dest_row, gates):
    seq_len, model_dim = residual.shape
    top_k = gates.shape[1]
    picked = jnp.take(returned.reshape(-1, model_dim), dest_row, axis=0, mode="fill", fill_value=0).reshape(seq_len, top_k, model_dim)
    mixed_sum = jnp.einsum("tk,tkd->td", gates, picked, preferred_element_type=jnp.float32)
    return (residual.astype(jnp.float32) + mixed_sum).astype(jnp.bfloat16)


def expert_ffn(received, w_gate, w_up, w_down):
    gate_act = jnp.einsum("pecd,edf->pecf", received, w_gate, preferred_element_type=jnp.float32)
    up_act = jnp.einsum("pecd,edf->pecf", received, w_up, preferred_element_type=jnp.float32)
    hidden = (jax.nn.silu(gate_act) * up_act).astype(jnp.bfloat16)
    return jnp.einsum("pecf,efd->pecd", hidden, w_down, preferred_element_type=jnp.float32).astype(jnp.bfloat16)


def moe_layer(tokens, experts, slots, gates, attn_gain, w_query, w_key, w_value, w_out, moe_gain, w_gate, w_up, w_down, group):
    seq_len, model_dim = tokens.shape
    local_experts = w_gate.shape[0]
    experts_total = local_experts * group
    capacity = capacity_of(seq_len, experts.shape[1], experts_total)
    residual = attention_block(tokens, attn_gain, w_query, w_key, w_value, w_out)
    normed = rms_norm(residual, moe_gain)
    dest_row = jnp.where(slots >= 0, experts * capacity + slots, experts_total * capacity).reshape(-1)
    dispatched = dispatch_rows(normed, dest_row, experts_total, capacity)
    received = lax.all_to_all(dispatched, "ep", 0, 0, tiled=True).reshape(group, local_experts, capacity, model_dim)
    expert_out = expert_ffn(received, w_gate, w_up, w_down).reshape(experts_total, capacity, model_dim)
    returned = lax.all_to_all(expert_out, "ep", 0, 0, tiled=True)
    return combine_rows(residual, returned, dest_row, gates)


def solution(mesh):
    group = mesh.shape["ep"]
    row_spec = P(("dp", "ep"), None)
    full_spec = P(None, None, None)
    gain_spec = P(None)
    expert_spec = P("ep", None, None)
    in_specs = (row_spec, row_spec, row_spec, row_spec, row_spec, row_spec, row_spec, row_spec, gain_spec, full_spec, full_spec, full_spec, full_spec, gain_spec, expert_spec, expert_spec, expert_spec)

    def device_fn(tokens_a, experts_a, slots_a, gates_a, tokens_b, experts_b, slots_b, gates_b, attn_gain, w_query, w_key, w_value, w_out, moe_gain, w_gate, w_up, w_down):
        out_a = moe_layer(tokens_a, experts_a, slots_a, gates_a, attn_gain, w_query, w_key, w_value, w_out, moe_gain, w_gate, w_up, w_down, group)
        out_b = moe_layer(tokens_b, experts_b, slots_b, gates_b, attn_gain, w_query, w_key, w_value, w_out, moe_gain, w_gate, w_up, w_down, group)
        return out_a, out_b

    return jax.shard_map(device_fn, mesh=mesh, in_specs=in_specs, out_specs=(row_spec, row_spec), check_vma=False)
```

profile of v0, /device:TPU:0, one launch (start us, length us, event | category | flops | bytes accessed | tf_op | source)
XLA Modules:
  0.0 109.3 jit_solution(17203426182509669265)
XLA Ops:
  0.6 0.0 copy-start.1
  0.7 0.0 slice-start.4
  0.7 0.8 convert_element_type.103
  1.5 1.5 %fusion.81 = f32[32]{0:T(128)S(1)} fusion(bf16[32,1536]{1,0:T(8,128)(2,1)} %param.25), kind=kLoop, calls=%fused_computation.83 | loop fusion | flops 147424 | bytes 98432 | tf_op jit(solution)/shard_map/reduce_sum | solution.py:12
  3.0 0.0 copy-start.2
  3.0 0.0 slice-start.5
  3.0 5.0 %convolution_convert_fusion.2 = bf16[32,24,64]{2,0,1:T(8,128)(2,1)S(1)} fusion(bf16[1536,24,64]{0,2,1:T(8,128)(2,1)} %param.31, bf16[32,1536]{1,0:T(8,128)(2,1)} %param.25, f32[32]{0:T(128)S(1)} %add_rsqrt_fusion.1, f32[1536]{0:T(1024)S(1)} %convert_element_type.103), kind=kOutput, calls=%fused_computation.50 | convolution fusion | flops 151240704 | bytes 4921472 | tf_op jit(solution)/shard_map/td,dhe->the/dot_general | solution.py:20
  8.1 2.2 %fusion.114 = bf16[32,24,64]{2,0,1:T(8,128)(2,1)S(1)} fusion(bf16[1536,24,64]{0,2,1:T(8,128)(2,1)S(1)} %copy-done, bf16[32,1536]{1,0:T(8,128)(2,1)S(1)} %copy-done.1, f32[32]{0:T(128)S(1)} %add_rsqrt_fusion.1, f32[1536]{0:T(1024)S(1)} %convert_element_type.103), kind=kOutput, calls=%fused_computation.134 | convolution fusion | flops 151191552 | bytes 4921472 | tf_op jit(solution)/shard_map/td,dhe->the/dot_general | solution.py:21
  10.3 0.1 fusion.78
  10.5 0.0 copy-start.4
  10.5 2.2 %convolution_convert_fusion.4 = bf16[32,24,64]{2,0,1:T(8,128)(2,1)S(1)} fusion(bf16[1536,24,64]{0,2,1:T(8,128)(2,1)S(1)} %bitcast.158, bf16[32,1536]{1,0:T(8,128)(2,1)S(1)} %copy-done.2, f32[1536]{0:T(1024)S(1)} %convert_element_type.103, f32[32]{0:T(128)S(1)} %add_rsqrt_fusion.3), kind=kOutput, calls=%fused_computation.52 | convolution fusion | flops 151240704 | bytes 4921472 | tf_op jit(solution)/shard_map/td,dhe->the/dot_general | solution.py:20
  12.8 2.2 %fusion.109 = bf16[32,24,64]{2,0,1:T(8,128)(2,1)S(1)} fusion(bf16[1536,24,64]{0,2,1:T(8,128)(2,1)S(1)} %copy-done, bf16[32,1536]{1,0:T(8,128)(2,1)S(1)} %copy-done.2, f32[1536]{0:T(1024)S(1)} %convert_element_type.103, f32[32]{0:T(128)S(1)} %add_rsqrt_fusion.3), kind=kOutput, calls=%fused_computation.133 | convolution fusion | flops 151191552 | bytes 4921472 | tf_op jit(solution)/shard_map/td,dhe->the/dot_general | solution.py:21
  15.1 0.1 copy.23
  15.1 0.1 reshape.162
  15.2 1.4 %scatter_custom_fusion.1 = s32[320]{0:T(512)S(1)} fusion(s32[256]{0:T(256)S(1)} %bitcast.166, s32[256]{0:T(256)S(1)} %and_select_fusion, s32[]{:T(128)} %constant.61.clone.1), kind=kCustom, calls=%fused_computation.121 | custom fusion | bytes 1284 | tf_op jit(solution)/shard_map/scatter | solution.py:39
  16.7 4.7 %fusion.61 = f32[24,32,32]{1,2,0:T(8,128)S(1)} fusion(bf16[32,24,64]{2,0,1:T(8,128)(2,1)S(1)} %convolution_convert_fusion.2, bf16[1536,24,64]{0,2,1:T(8,128)(2,1)} %param.30, pred[32,32]{0,1:T(8,128)(4,1)S(1)} %iota_compare_fusion, bf16[32,1536]{1,0:T(8,128)(2,1)S(1)} %copy-done.1, f32[32]{0:T(128)S(1)} %add_rsqrt_fusion.1, f32[1536]{0:T(1024)S(1)} %convert_element_type.103), kind=kOutput, calls=%fused_computation.47 | convolution fusion | flops 154435584 | bytes 5020800 | tf_op jit(solution)/shard_map/qhe,khe->hqk/dot_general | solution.py:22
  21.4 0.1 fusion.117
  21.5 0.1 copy.56
  21.6 4.7 %fusion.60 = f32[24,32,32]{1,2,0:T(8,128)S(1)} fusion(bf16[32,24,64]{2,0,1:T(8,128)(2,1)S(1)} %convolution_convert_fusion.4, bf16[1536,24,64]{0,2,1:T(8,128)(2,1)} %param.30, pred[32,32]{0,1:T(8,128)(4,1)S(1)} %iota_compare_fusion, bf16[32,1536]{1,0:T(8,128)(2,1)S(1)} %copy-done.2, f32[1536]{0:T(1024)S(1)} %convert_element_type.103, f32[32]{0:T(128)S(1)} %add_rsqrt_fusion.3), kind=kOutput, calls=%fused_computation.46 | convolution fusion | flops 154435584 | bytes 5020800 | tf_op jit(solution)/shard_map/qhe,khe->hqk/dot_general | solution.py:22
  26.3 0.1 fusion.116
  26.4 0.1 copy.57
  26.6 3.6 %multiply_reduce_fusion = (f32[32]{0:T(128)S(1)}, f32[32,1536]{1,0:T(8,128)S(1)}) fusion(bf16[24,64,1536]{2,1,0:T(8,128)(2,1)} %param.33, bf16[32,24,64]{2,1,0:T(8,128)(2,1)S(1)} %copy.56, f32[24,32]{1,0:T(8,128)S(1)} %fusion.117, f32[24,32,32]{1,2,0:T(8,128)S(1)} %fusion.61, bf16[32,1536]{1,0:T(8,128)(2,1)S(1)} %copy-done.1), kind=kOutput, calls=%fused_computation.93 | convolution fusion | flops 154559232 | bytes 5213312 | tf_op jit(solution)/shard_map/qhe,hed->qd/dot_general | solution.py:27
  30.2 3.6 %multiply_reduce_fusion.1 = (f32[32]{0:T(128)S(1)}, f32[32,1536]{1,0:T(8,128)S(1)}) fusion(bf16[24,64,1536]{2,1,0:T(8,128)(2,1)} %param.33, bf16[32,24,64]{2,1,0:T(8,128)(2,1)S(1)} %copy.57, f32[24,32]{1,0:T(8,128)S(1)} %fusion.116, f32[24,32,32]{1,2,0:T(8,128)S(1)} %fusion.60, bf16[32,1536]{1,0:T(8,128)(2,1)S(1)} %copy-done.2), kind=kOutput, calls=%fused_computation.96 | convolution fusion | flops 154559232 | bytes 5213312 | tf_op jit(solution)/shard_map/qhe,hed->qd/dot_general | solution.py:27
  33.8 0.1 multiply_convert_fusion
  34.0 0.0 copy-start.6
  34.0 2.2 %gather_fusion.2 = bf16[320,1536]{1,0:T(8,128)(2,1)S(1)} fusion(bf16[32,1536]{1,0:T(8,128)(2,1)S(1)} %get-tuple-element.4, s32[1024]{0:T(1024)S(1)} %pad_clamp_fusion.1), kind=kCustom, calls=%fused_computation.2.clone | custom fusion | bytes 1967360 | tf_op jit(solution)/shard_map/jit(_take)/gather | solution.py:40
  36.2 1.1 %select_bitcast_fusion = bf16[40,8,1536]{2,1,0:T(8,128)(2,1)} fusion(bf16[320,1536]{1,0:T(8,128)(2,1)S(1)} %gather_fusion.2, pred[320]{0:T(512)(128)(4,1)S(1)} %compare_and_fusion.1), kind=kLoop, calls=%fused_computation.56 | loop fusion | flops 491520 | bytes 1966400 | tf_op jit(solution)/shard_map/reshape | solution.py:40
  37.3 4.3 %all-to-all-start.2 = ((bf16[40,8,1536]{2,1,0:T(8,128)(2,1)}), bf16[40,8,1536]{2,1,0:T(8,128)(2,1)S(1)}, u32[]{:S(2)}, u32[]{:S(2)}) async-start(bf16[40,8,1536]{2,1,0:T(8,128)(2,1)} %select_bitcast_fusion), calls=%async_computation.2 | async-start | bytes 1966080 | tf_op jit(solution)/shard_map/all_to_all | solution.py:67
  41.6 0.1 reshape.167
  41.8 0.1 copy.19
  41.9 0.1 reshape.155
  42.0 0.1 reshape.160
  42.1 1.4 %scatter_custom_fusion = s32[320]{0:T(512)S(1)} fusion(s32[256]{0:T(256)S(1)} %bitcast.165, s32[256]{0:T(256)S(1)} %and_select_fusion, s32[]{:T(128)} %constant.61.clone.1), kind=kCustom, calls=%fused_computation.123 | custom fusion | bytes 1284 | tf_op jit(solution)/shard_map/scatter | solution.py:39
  43.5 2.2 %gather_fusion = bf16[320,1536]{1,0:T(8,128)(2,1)S(1)} fusion(bf16[32,1536]{1,0:T(8,128)(2,1)S(1)} %get-tuple-element.5, s32[1024]{0:T(1024)S(1)} %pad_clamp_fusion.3), kind=kCustom, calls=%fused_computation.clone | custom fusion | bytes 1967360 | tf_op jit(solution)/shard_map/jit(_take)/gather | solution.py:40
  45.8 1.1 select_bitcast_fusion.1
  46.9 9.4 %all-to-all-done.2 = bf16[40,8,1536]{2,1,0:T(8,128)(2,1)S(1)} async-done(((bf16[40,8,1536]{2,1,0:T(8,128)(2,1)}), bf16[40,8,1536]{2,1,0:T(8,128)(2,1)S(1)}, u32[]{:S(2)}, u32[]{:S(2)}) %all-to-all-start.2) | async-done | bytes 983072 | tf_op jit(solution)/shard_map/all_to_all | solution.py:67
  56.3 2.3 %all-to-all-start = ((bf16[40,8,1536]{2,1,0:T(8,128)(2,1)}), bf16[40,8,1536]{2,1,0:T(8,128)(2,1)S(1)}, u32[]{:S(2)}, u32[]{:S(2)}) async-start(bf16[40,8,1536]{2,1,0:T(8,128)(2,1)} %select_bitcast_fusion.1), calls=%async_computation | async-start | bytes 1966080 | tf_op jit(solution)/shard_map/all_to_all | solution.py:67
  58.6 0.0 slice-start
  58.6 4.9 %fusion.35 = f32[8,5,8,512]{3,2,0,1:T(8,128)S(1)} fusion(bf16[5,1536,512]{2,1,0:T(8,128)(2,1)} %param.35, bf16[8,5,8,1536]{3,2,1,0:T(8,128)(2,1)S(1)} %bitcast.159), kind=kOutput, calls=%fused_computation.33 | convolution fusion | flops 503316480 | bytes 9502720 | tf_op jit(solution)/shard_map/pecd,edf->pecf/dot_general | solution.py:52
  63.5 0.0 slice-start.1
  63.5 4.8 %fusion.55 = bf16[8,5,8,512]{3,2,0,1:T(8,128)(2,1)S(1)} fusion(bf16[5,1536,512]{2,1,0:T(8,128)(2,1)} %param.36, bf16[8,5,8,1536]{3,2,1,0:T(8,128)(2,1)S(1)} %bitcast.160, f32[8,5,8,512]{3,2,0,1:T(8,128)S(1)} %fusion.35), kind=kOutput, calls=%fused_computation.41 | convolution fusion | flops 504299520 | bytes 9830400 | tf_op jit(solution)/shard_map/pecd,edf->pecf/dot_general | solution.py:53
  68.3 1.5 %fusion.20 = bf16[8,5,8,1536]{3,2,0,1:T(8,128)(2,1)S(1)} fusion(bf16[8,5,8,512]{3,2,0,1:T(8,128)(2,1)S(1)} %fusion.55, bf16[5,512,1536]{2,1,0:T(8,128)(2,1)S(1)} %bitcast.154), kind=kOutput, calls=%fused_computation.22 | convolution fusion | flops 503808000 | bytes 9175040 | tf_op jit(solution)/shard_map/pecf,efd->pecd/dot_general | solution.py:55
  69.8 1.0 copy.26
  70.9 2.3 %all-to-all-done = bf16[40,8,1536]{2,1,0:T(8,128)(2,1)S(1)} async-done(((bf16[40,8,1536]{2,1,0:T(8,128)(2,1)}), bf16[40,8,1536]{2,1,0:T(8,128)(2,1)S(1)}, u32[]{:S(2)}, u32[]{:S(2)}) %all-to-all-start) | async-done | bytes 983072 | tf_op jit(solution)/shard_map/all_to_all | solution.py:67
  73.2 2.3 %all-to-all-start.3 = ((bf16[40,8,1536]{2,1,0:T(8,128)(2,1)}), bf16[40,8,1536]{2,1,0:T(8,128)(2,1)S(1)}, u32[]{:S(2)}, u32[]{:S(2)}) async-start(bf16[40,8,1536]{2,1,0:T(8,128)(2,1)} %bitcast.32), calls=%async_computation.3 | async-start | bytes 1966080 | tf_op jit(solution)/shard_map/all_to_all | solution.py:69
  75.5 0.0 slice-start.2
  75.5 4.9 %fusion.32 = f32[8,5,8,512]{3,2,0,1:T(8,128)S(1)} fusion(bf16[5,1536,512]{2,1,0:T(8,128)(2,1)} %param.35, bf16[8,5,8,1536]{3,2,1,0:T(8,128)(2,1)S(1)} %bitcast.161), kind=kOutput, calls=%fused_computation.32 | convolution fusion | flops 503316480 | bytes 9502720 | tf_op jit(solution)/shard_map/pecd,edf->pecf/dot_general | solution.py:52
  80.3 0.0 slice-start.3
  80.4 4.8 %fusion.52 = bf16[8,5,8,512]{3,2,0,1:T(8,128)(2,1)S(1)} fusion(bf16[5,1536,512]{2,1,0:T(8,128)(2,1)} %param.36, bf16[8,5,8,1536]{3,2,1,0:T(8,128)(2,1)S(1)} %bitcast.162, f32[8,5,8,512]{3,2,0,1:T(8,128)S(1)} %fusion.32), kind=kOutput, calls=%fused_computation.40 | convolution fusion | flops 504299520 | bytes 9830400 | tf_op jit(solution)/shard_map/pecd,edf->pecf/dot_general | solution.py:53
  85.2 0.0 copy-start.8
  85.2 0.0 copy-start.9
  85.2 1.5 %fusion.23 = bf16[8,5,8,1536]{3,2,0,1:T(8,128)(2,1)S(1)} fusion(bf16[8,5,8,512]{3,2,0,1:T(8,128)(2,1)S(1)} %fusion.52, bf16[5,512,1536]{2,1,0:T(8,128)(2,1)S(1)} %bitcast.156), kind=kOutput, calls=%fused_computation.23 | convolution fusion | flops 503808000 | bytes 9175040 | tf_op jit(solution)/shard_map/pecf,efd->pecd/dot_general | solution.py:55
  86.7 1.0 copy.22
  87.7 2.3 %all-to-all-done.3 = bf16[40,8,1536]{2,1,0:T(8,128)(2,1)S(1)} async-done(((bf16[40,8,1536]{2,1,0:T(8,128)(2,1)}), bf16[40,8,1536]{2,1,0:T(8,128)(2,1)S(1)}, u32[]{:S(2)}, u32[]{:S(2)}) %all-to-all-start.3) | async-done | bytes 983072 | tf_op jit(solution)/shard_map/all_to_all | solution.py:69
  90.1 2.3 %all-to-all-start.1 = ((bf16[40,8,1536]{2,1,0:T(8,128)(2,1)}), bf16[40,8,1536]{2,1,0:T(8,128)(2,1)S(1)}, u32[]{:S(2)}, u32[]{:S(2)}) async-start(bf16[40,8,1536]{2,1,0:T(8,128)(2,1)} %bitcast.15), calls=%async_computation.1 | async-start | bytes 1966080 | tf_op jit(solution)/shard_map/all_to_all | solution.py:69
  92.4 0.1 copy.36
  92.5 0.1 copy.32
  92.6 1.3 %gather_fusion.3 = bf16[256,1536]{1,0:T(8,128)(2,1)S(1)} fusion(bf16[320,1536]{1,0:T(8,128)(2,1)S(1)} %bitcast.151, s32[1024]{0:T(1024)S(1)} %pad_clamp_fusion), kind=kCustom, calls=%fused_computation.3.clone | custom fusion | bytes 1573888 | tf_op jit(solution)/shard_map/jit(_take)/gather | solution.py:46
  93.8 0.4 fusion.68
  94.3 0.7 fusion.84
  94.9 12.0 %all-to-all-done.1 = bf16[40,8,1536]{2,1,0:T(8,128)(2,1)S(1)} async-done(((bf16[40,8,1536]{2,1,0:T(8,128)(2,1)}), bf16[40,8,1536]{2,1,0:T(8,128)(2,1)S(1)}, u32[]{:S(2)}, u32[]{:S(2)}) %all-to-all-start.1) | async-done | bytes 983072 | tf_op jit(solution)/shard_map/all_to_all | solution.py:69
  106.9 1.3 %gather_fusion.1 = bf16[256,1536]{1,0:T(8,128)(2,1)S(1)} fusion(bf16[320,1536]{1,0:T(8,128)(2,1)S(1)} %bitcast.152, s32[1024]{0:T(1024)S(1)} %pad_clamp_fusion.2), kind=kCustom, calls=%fused_computation.1.clone | custom fusion | bytes 1573888 | tf_op jit(solution)/shard_map/jit(_take)/gather | solution.py:46
  108.2 0.4 fusion.70
  108.6 0.7 fusion.85
  (45 shorter events, 0.2 us)
Async XLA Ops:
  0.6 7.4 %copy-start.1 = (bf16[32,1536]{1,0:T(8,128)(2,1)S(1)}, bf16[32,1536]{1,0:T(8,128)(2,1)}, u32[]{:S(2)}) copy-start(bf16[32,1536]{1,0:T(8,128)(2,1)} %param.25) | copy-start | bytes 294916
  0.6 7.4 %copy-start = (bf16[1536,24,64]{0,2,1:T(8,128)(2,1)S(1)}, bf16[1536,24,64]{0,2,1:T(8,128)(2,1)}, u32[]{:S(2)}) copy-start(bf16[1536,24,64]{0,2,1:T(8,128)(2,1)} %param.32) | copy-start | bytes 14155780
  0.7 9.8 %slice-start.4 = ((s8[4718592]{0:T(1024)(128)(4,1)}), s8[4194304]{0:T(1024)(128)(4,1)S(1)}, s32[]{:S(2)}) async-start(s8[4718592]{0:T(1024)(128)(4,1)} %bitcast.157), calls=%async_computation.8 | async-start | bytes 8388608
  3.0 7.3 %copy-start.2 = (bf16[32,1536]{1,0:T(8,128)(2,1)S(1)}, bf16[32,1536]{1,0:T(8,128)(2,1)}, u32[]{:S(2)}) copy-start(bf16[32,1536]{1,0:T(8,128)(2,1)} %param.21) | copy-start | bytes 294916
  3.0 7.4 %slice-start.5 = ((s8[4718592]{0:T(1024)(128)(4,1)}), s8[524288]{0:T(1024)(128)(4,1)S(1)}, s32[]{:S(2)}) async-start(s8[4718592]{0:T(1024)(128)(4,1)} %bitcast.157), calls=%async_computation.9 | async-start | bytes 1048576
  10.5 4.5 %copy-start.3 = (s32[32,8]{0,1:T(8,128)S(1)}, s32[32,8]{0,1:T(8,128)}, u32[]{:S(2)}) copy-start(s32[32,8]{0,1:T(8,128)} %param.27) | copy-start | bytes 3076
  10.5 4.5 %copy-start.4 = (s32[32,8]{0,1:T(8,128)S(1)}, s32[32,8]{0,1:T(8,128)}, u32[]{:S(2)}) copy-start(s32[32,8]{0,1:T(8,128)} %param.26) | copy-start | bytes 3076
  21.4 5.2 %copy-start.5 = (bf16[1536]{0:T(1024)(128)(2,1)S(1)}, bf16[1536]{0:T(1024)(128)(2,1)}, u32[]{:S(2)}) copy-start(bf16[1536]{0:T(1024)(128)(2,1)} %param.34) | copy-start | bytes 9220
  34.0 7.8 %copy-start.6 = (s32[32,8]{0,1:T(8,128)S(1)}, s32[32,8]{0,1:T(8,128)}, u32[]{:S(2)}) copy-start(s32[32,8]{0,1:T(8,128)} %param.23) | copy-start | bytes 3076
  34.0 7.8 %copy-start.7 = (s32[32,8]{0,1:T(8,128)S(1)}, s32[32,8]{0,1:T(8,128)}, u32[]{:S(2)}) copy-start(s32[32,8]{0,1:T(8,128)} %param.22) | copy-start | bytes 3076
  37.3 19.0 %all-to-all-start.2 = ((bf16[40,8,1536]{2,1,0:T(8,128)(2,1)}), bf16[40,8,1536]{2,1,0:T(8,128)(2,1)S(1)}, u32[]{:S(2)}, u32[]{:S(2)}) async-start(bf16[40,8,1536]{2,1,0:T(8,128)(2,1)} %select_bitcast_fusion), calls=%async_computation.2 | async-start | bytes 1966080 | tf_op jit(solution)/shard_map/all_to_all | solution.py:67
  56.3 16.9 %all-to-all-start = ((bf16[40,8,1536]{2,1,0:T(8,128)(2,1)}), bf16[40,8,1536]{2,1,0:T(8,128)(2,1)S(1)}, u32[]{:S(2)}, u32[]{:S(2)}) async-start(bf16[40,8,1536]{2,1,0:T(8,128)(2,1)} %select_bitcast_fusion.1), calls=%async_computation | async-start | bytes 1966080 | tf_op jit(solution)/shard_map/all_to_all | solution.py:67
  58.6 9.7 %slice-start = ((s8[7864320]{0:T(1024)(128)(4,1)}), s8[4194304]{0:T(1024)(128)(4,1)S(1)}, s32[]{:S(2)}) async-start(s8[7864320]{0:T(1024)(128)(4,1)} %bitcast.153), calls=%async_computation.4 | async-start | bytes 8388608
  63.5 4.8 %slice-start.1 = ((s8[7864320]{0:T(1024)(128)(4,1)}), s8[3670016]{0:T(1024)(128)(4,1)S(1)}, s32[]{:S(2)}) async-start(s8[7864320]{0:T(1024)(128)(4,1)} %bitcast.153), calls=%async_computation.5 | async-start | bytes 7340032
  73.2 16.9 %all-to-all-start.3 = ((bf16[40,8,1536]{2,1,0:T(8,128)(2,1)}), bf16[40,8,1536]{2,1,0:T(8,128)(2,1)S(1)}, u32[]{:S(2)}, u32[]{:S(2)}) async-start(bf16[40,8,1536]{2,1,0:T(8,128)(2,1)} %bitcast.32), calls=%async_computation.3 | async-start | bytes 1966080 | tf_op jit(solution)/shard_map/all_to_all | solution.py:69
  75.5 9.7 %slice-start.2 = ((s8[7864320]{0:T(1024)(128)(4,1)}), s8[4194304]{0:T(1024)(128)(4,1)S(1)}, s32[]{:S(2)}) async-start(s8[7864320]{0:T(1024)(128)(4,1)} %bitcast.155), calls=%async_computation.6 | async-start | bytes 8388608
  80.3 4.8 %slice-start.3 = ((s8[7864320]{0:T(1024)(128)(4,1)}), s8[3670016]{0:T(1024)(128)(4,1)S(1)}, s32[]{:S(2)}) async-start(s8[7864320]{0:T(1024)(128)(4,1)} %bitcast.155), calls=%async_computation.7 | async-start | bytes 7340032
  85.2 7.2 %copy-start.8 = (bf16[32,8]{0,1:T(8,128)(2,1)S(1)}, bf16[32,8]{0,1:T(8,128)(2,1)}, u32[]{:S(2)}) copy-start(bf16[32,8]{0,1:T(8,128)(2,1)} %param.28) | copy-start | bytes 1540
  85.2 7.2 %copy-start.9 = (bf16[32,8]{0,1:T(8,128)(2,1)S(1)}, bf16[32,8]{0,1:T(8,128)(2,1)}, u32[]{:S(2)}) copy-start(bf16[32,8]{0,1:T(8,128)(2,1)} %param.24) | copy-start | bytes 1540
  90.1 16.9 %all-to-all-start.1 = ((bf16[40,8,1536]{2,1,0:T(8,128)(2,1)}), bf16[40,8,1536]{2,1,0:T(8,128)(2,1)S(1)}, u32[]{:S(2)}, u32[]{:S(2)}) async-start(bf16[40,8,1536]{2,1,0:T(8,128)(2,1)} %bitcast.15), calls=%async_computation.1 | async-start | bytes 1966080 | tf_op jit(solution)/shard_map/all_to_all | solution.py:69
where the time goes:
time: 110 us; the launch traced here: 109 us
  matrix products  51.6 us (47%)
  waiting for transfers between devices  26.1 us (24%)
  local copies, waits for them, and re-layouts  12.8 us (12%)
  starting transfers between devices  11.2 us (10%)
  other arithmetic  6.47 us (6%)
  between operations  1.22 us (1%)
    all_to_all x2, waiting for transfers between devices, moe_layer(): returned = lax.all_to_all(expert_out, 'ep', 0, 0, tiled=True)  14.3 us
    all_to_all x2, waiting for transfers between devices, moe_layer(): lax.all_to_all(dispatched, 'ep', 0, 0, tiled=True)  11.8 us
    dot_general x2, matrix products, expert_ffn(): jnp.einsum('pecd,edf->pecf', received, w_gate, preferred_element_type=jnp...  9.71 us
    dot_general x2, matrix products, expert_ffn(): jnp.einsum('pecd,edf->pecf', received, w_up, preferred_element_type=jnp.f...  9.65 us
    dot_general x2, matrix products, attention_block(): jnp.einsum('qhe,khe->hqk', query, keys, preferred_element_type=jnp.float32)  9.44 us
    dot_general x2, matrix products, attention_block(): jnp.einsum('qhe,hed->qd', context, w_out, preferred_element_type=jnp.floa...  7.26 us
    dot_general x2, matrix products, attention_block(): jnp.einsum('td,dhe->the', normed, w_key, preferred_element_type=jnp.float32)  7.23 us
    all_to_all x2, starting transfers between devices, moe_layer(): lax.all_to_all(dispatched, 'ep', 0, 0, tiled=True)  6.6 us
  transfers between devices with their start and end apart: 4, of which 4 were waited for; matrix products, arithmetic and copies ran while one was open for 29% of the time, Pallas kernels for 0%

commit v1 on v0

v1 whole, which is shorter than its diff:
```python
import functools

import jax
import jax.numpy as jnp
from jax import lax
from jax.experimental import pallas as pl
from jax.experimental.pallas import tpu as pltpu
from jax.sharding import PartitionSpec as P

NORM_EPS = 1e-6
MASK_VALUE = -1e30
MESH = pl.DeviceIdType.MESH

GROUP = 8
TOKENS = 32
DIM = 1536
FFN = 512
LOCAL = 5
SLOTS = 8
HALF = DIM // 2
CHUNK = 256
CHUNKS = DIM // CHUNK
ROWS = GROUP * TOKENS
LROWS = LOCAL * GROUP * SLOTS
F32 = jnp.float32
BF16 = jnp.bfloat16

NT = (((1,), (1,)), ((), ()))
TN = (((0,), (0,)), ((), ()))


def rms_rows(rows_f, gain):
    inv = lax.rsqrt(jnp.mean(rows_f * rows_f, axis=-1, keepdims=True) + NORM_EPS)
    return (rows_f * inv * gain).astype(BF16)


def kernel(
    tok_a, exp_a, slot_a, gate_a, tok_b, exp_b, slot_b, gate_b,
    again_hbm, wq_hbm, wk_hbm, wv_hbm, wo_hbm, mgain_hbm, wg_hbm, wu_hbm, wd_hbm,
    out_a, out_b,
    xv, gains, ev, sv, gv,
    wqkv, wov, wgv, wuv, wdv,
    norm_a, qkv, ctx, hv, uall, meta, disp, comb, picked, o2, part, r1, s2, r2, fin, r3, yv,
    sem_in, sem_qkv, sem_o, sem_exp, sem_out,
    msend, mrecv, dsend, drecv, osend, orecv, rsend, rrecv,
):
    me = lax.axis_index("ep")
    core = me % 2
    px = (me // 2) % 2
    py = me // 4
    flip1 = me + 1 - 2 * core
    flip2 = me + 2 - 4 * px
    flip4 = me + 4 - 8 * py
    flip = {
        1: flip1,
        2: flip2,
        4: flip4,
        3: flip2 + 1 - 2 * core,
        5: flip4 + 1 - 2 * core,
        6: flip2 + 4 - 8 * py,
    }
    flip[7] = flip[6] + 1 - 2 * core
    first = (1 - core) * flip2 + core * flip4
    second = (1 - core) * flip4 + core * flip2

    def local(src, dst, sem):
        return pltpu.make_async_copy(src, dst, sem)

    def remote(src, dst, ssem, rsem, dev):
        return pltpu.make_async_remote_copy(
            src_ref=src, dst_ref=dst, send_sem=ssem, recv_sem=rsem,
            device_id={"ep": dev}, device_id_type=MESH,
        )

    small = [
        local(exp_a, ev.at[0], sem_in.at[0]),
        local(exp_b, ev.at[1], sem_in.at[1]),
        local(slot_a, sv.at[0], sem_in.at[2]),
        local(slot_b, sv.at[1], sem_in.at[3]),
        local(gate_a, gv.at[0], sem_in.at[4]),
        local(gate_b, gv.at[1], sem_in.at[5]),
        local(tok_a, xv.at[pl.ds(0, TOKENS)], sem_in.at[6]),
        local(tok_b, xv.at[pl.ds(TOKENS, TOKENS)], sem_in.at[7]),
        local(again_hbm, gains.at[0], sem_in.at[8]),
        local(mgain_hbm, gains.at[1], sem_in.at[9]),
    ]
    for copy in small:
        copy.start()

    whbm = (wq_hbm, wk_hbm, wv_hbm)

    def qkv_copy(which, c):
        rows = pl.ds(pl.multiple_of(c * CHUNK, CHUNK), CHUNK)
        return local(whbm[which].at[rows], wqkv.at[which, c], sem_qkv.at[which, c])

    for c in range(CHUNKS):
        for which in range(3):
            qkv_copy(which, c).start()
    wo_copy = local(wo_hbm, wov, sem_o)
    wo_copy.start()

    barrier = pltpu.get_barrier_semaphore()
    for k in range(1, GROUP):
        pl.semaphore_signal(barrier, inc=1, device_id={"ep": flip[k]}, device_id_type=MESH)

    for copy in small[:6]:
        copy.wait()

    lane = lax.broadcasted_iota(jnp.int32, (SLOTS, 128), 1)
    my_lanes = lane // TOKENS == me % 4
    for b in range(2):
        code = jnp.where(sv[b] >= 0, ev[b] * SLOTS + sv[b], -1).astype(F32)
        code = jnp.concatenate([code] * 4, axis=1)
        gate = jnp.concatenate([gv[b].astype(F32)] * 4, axis=1)
        meta[me, b, 0] = jnp.where(my_lanes, code, -1.0)
        meta[me, b, 1] = jnp.where(my_lanes, gate, 0.0)

    pl.semaphore_wait(barrier, GROUP - 1)

    def meta_copy(k):
        return remote(meta.at[me], meta.at[me], msend.at[k], mrecv.at[k], flip[k])

    for k in range(1, GROUP):
        meta_copy(k).start()

    for copy in small[6:]:
        copy.wait()
    norm_a[...] = rms_rows(xv[...].astype(F32), gains[0].astype(F32))

    def qkv_step(c, carry):
        for which in range(3):
            qkv_copy(which, c).wait()
        for which in range(3):
            prod = lax.dot_general(norm_a[...], wqkv[which, c], NT, preferred_element_type=F32)
            qkv[which, c] = prod.astype(BF16)
        return carry

    lax.fori_loop(0, CHUNKS, qkv_step, 0)

    def expert_copies(e):
        return (
            local(wg_hbm.at[e], wgv.at[e], sem_exp.at[0, e]),
            local(wu_hbm.at[e], wuv.at[e], sem_exp.at[1, e]),
            local(wd_hbm.at[e], wdv.at[e], sem_exp.at[2, e]),
        )

    for e in range(LOCAL):
        for copy in expert_copies(e):
            copy.start()

    n2 = 2 * TOKENS
    lane128 = lax.broadcasted_iota(jnp.int32, (n2, 128), 1)
    row128 = lax.broadcasted_iota(jnp.int32, (n2, 128), 0)
    key = lane128 % n2
    visible = (key // TOKENS == row128 // TOKENS) & (key <= row128)
    low = lane128 < n2
    scale = 64.0 ** -0.5
    for pair in range(DIM // 128):
        c, off = pair // 2, (pair % 2) * 128
        q = qkv[0, c, :, off:off + 128]
        k = qkv[1, c, :, off:off + 128]
        v = qkv[2, c, :, off:off + 128]
        zero = jnp.zeros_like(k)
        kk = jnp.concatenate([jnp.where(low, k, zero), jnp.where(low, zero, k)], axis=0)
        vv = jnp.concatenate([jnp.where(low, v, zero), jnp.where(low, zero, v)], axis=0)
        s = lax.dot_general(q, kk, NT, preferred_element_type=F32) * scale
        s = jnp.where(visible, s, MASK_VALUE)
        m0 = jnp.max(jnp.where(low, s, -jnp.inf), axis=-1, keepdims=True)
        m1 = jnp.max(jnp.where(low, -jnp.inf, s), axis=-1, keepdims=True)
        p = jnp.exp(s - jnp.where(low, m0, m1))
        d0 = jnp.sum(jnp.where(low, p, 0.0), axis=-1, keepdims=True)
        d1 = jnp.sum(jnp.where(low, 0.0, p), axis=-1, keepdims=True)
        p = (p / jnp.where(low, d0, d1)).astype(BF16)
        ctx[:, pair * 128:(pair + 1) * 128] = jnp.dot(p, vv, preferred_element_type=F32).astype(BF16)

    wo_copy.wait()
    attn = jnp.dot(ctx[...], wov[...], preferred_element_type=F32)
    h = (xv[...].astype(F32) + attn).astype(BF16)
    hv[...] = h
    u = rms_rows(h.astype(F32), gains[1].astype(F32))
    my_rows = pl.ds(pl.multiple_of(me * TOKENS, TOKENS), TOKENS)
    uall[0, my_rows, :] = u[:TOKENS]
    uall[1, my_rows, :] = u[TOKENS:]

    def block(b, dev, lo=0, n=TOKENS):
        return uall.at[b, pl.ds(pl.multiple_of(dev * TOKENS + lo, 16), n)]

    def disp_copy(b, i, dev_block, target, slot, lo=0, n=TOKENS):
        ref = block(b, dev_block, lo, n)
        return remote(ref, ref, dsend.at[b, i], drecv.at[b, slot], target)

    H = TOKENS // 2

    def d_near_x(b):
        return disp_copy(b, 0, me, flip[2], 2)

    def d_near_y(b):
        return disp_copy(b, 1, me, flip[4], 4)

    def d_sib(b):
        return disp_copy(b, 2, me, flip[1], 1)

    def d_fwd_x(b):
        return disp_copy(b, 3, flip[2], flip[4], 6, 0, H)

    def d_fwd_y(b):
        return disp_copy(b, 4, flip[4], flip[2], 0, H, H)

    def d_sib_x(b):
        return disp_copy(b, 5, flip[2], flip[1], 3)

    def d_sib_y(b):
        return disp_copy(b, 6, flip[4], flip[1], 5)

    def d_sib_d(b):
        return disp_copy(b, 7, flip[6], flip[1], 7)

    def d_wait(b, slot, dev, lo=0, n=TOKENS):
        ref = block(b, dev, lo, n)
        remote(ref, ref, dsend.at[b, 0], drecv.at[b, slot], flip[1]).wait_recv()

    for b in range(2):
        d_near_x(b).start()
        d_near_y(b).start()
        d_sib(b).start()

    for k in range(1, GROUP):
        remote(meta.at[flip[k]], meta.at[flip[k]], msend.at[k], mrecv.at[k], flip[k]).wait_recv()

    slot_row = lax.broadcasted_iota(jnp.int32, (SLOTS, ROWS), 0)
    row64 = lax.broadcasted_iota(jnp.int32, (GROUP * SLOTS, ROWS), 0)
    lane64 = lax.broadcasted_iota(jnp.int32, (GROUP * SLOTS, ROWS), 1)
    owner_hit = lane64 // TOKENS == row64 // SLOTS
    for b in range(2):
        halves = []
        for kind in range(2):
            parts = []
            for side in range(2):
                acc = meta[4 * side, b, kind]
                for p in range(1, 4):
                    acc = jnp.maximum(acc, meta[4 * side + p, b, kind])
                parts.append(acc)
            halves.append(jnp.concatenate(parts, axis=1))
        code, gate = halves
        code_rows = [jnp.broadcast_to(code[j:j + 1], (SLOTS, ROWS)) for j in range(SLOTS)]
        gate_rows = [jnp.broadcast_to(gate[j:j + 1], (SLOTS, ROWS)) for j in range(SLOTS)]
        for who in range(2):
            dev = me if who == 0 else flip[1]
            for e in range(LOCAL):
                target = ((dev * LOCAL + e) * SLOTS + slot_row).astype(F32)
                hit = jnp.zeros((SLOTS, ROWS), F32)
                weight = jnp.zeros((SLOTS, ROWS), F32)
                for j in range(SLOTS):
                    match = code_rows[j] == target
                    weight = weight + jnp.where(match, gate_rows[j], 0.0)
                    if who == 0:
                        hit = hit + jnp.where(match, 1.0, 0.0)
                rows = slice((who * LOCAL + e) * 64, (who * LOCAL + e + 1) * 64)
                wide = jnp.concatenate([weight] * GROUP, axis=0)
                comb[b, rows, :] = jnp.where(owner_hit, wide, 0.0).astype(BF16)
                if who == 0:
                    wide = jnp.concatenate([hit] * GROUP, axis=0)
                    disp[b, e * 64:(e + 1) * 64, :] = jnp.where(owner_hit, wide, 0.0).astype(BF16)

    def relay(b):
        d_wait(b, 2, flip[2])
        d_fwd_x(b).start()
        d_sib_x(b).start()
        d_wait(b, 4, flip[4])
        d_fwd_y(b).start()
        d_sib_y(b).start()

    def relay_far(b):
        d_wait(b, 6, flip[6], 0, H)
        d_wait(b, 0, flip[6], H, H)
        d_sib_d(b).start()

    def gathered(b):
        d_wait(b, 1, flip[1])
        d_wait(b, 3, flip[3])
        d_wait(b, 5, flip[5])
        d_wait(b, 7, flip[7])

    def pick(b):
        def pick_step(n, carry):
            cols = pl.ds(pl.multiple_of(n * CHUNK, CHUNK), CHUNK)
            picked[:, cols] = jnp.dot(disp[b], uall[b, :, cols], preferred_element_type=F32).astype(BF16)
            return carry

        lax.fori_loop(0, CHUNKS, pick_step, 0)

    def experts(b):
        def expert_step(e, carry):
            if b == 0:
                for copy in expert_copies(e):
                    copy.wait()
            rows = pl.ds(pl.multiple_of(e * 64, 64), 64)
            x = picked[rows, :]
            g = jnp.dot(x, wgv[e], preferred_element_type=F32)
            up = jnp.dot(x, wuv[e], preferred_element_type=F32)
            hidden = (g * (1.0 / (1.0 + jnp.exp(-g))) * up).astype(BF16)
            o = jnp.dot(hidden, wdv[e], preferred_element_type=F32).astype(BF16)
            o2[b, 0, rows, :] = o[:, :HALF]
            o2[b, 1, rows, :] = o[:, HALF:]
            return carry

        lax.fori_loop(0, LOCAL, expert_step, 0)

    def o_copy(b):
        src = o2.at[b, 1 - core, pl.ds(0, LROWS)]
        dst = o2.at[b, 1 - core, pl.ds(LROWS, LROWS)]
        return remote(src, dst, osend.at[b], orecv.at[b], flip[1])

    def o_wait(b):
        ref = o2.at[b, core, pl.ds(LROWS, LROWS)]
        remote(ref, ref, osend.at[b], orecv.at[b], flip[1]).wait_recv()

    def combine(b):
        for n in range(HALF // CHUNK):
            cols = slice(n * CHUNK, (n + 1) * CHUNK)
            part[b, :, cols] = lax.dot_general(comb[b], o2[b, core, :, cols], TN, preferred_element_type=F32)

    def chip_rows(ref, b, dev):
        return ref.at[b, pl.ds(pl.multiple_of((dev // 2) * 64, 64), 64)]

    def far_copy(b):
        return remote(chip_rows(part, b, flip[6]), r1.at[b, 1], rsend.at[b, 0], rrecv.at[b, 0], first)

    def near_copy(b):
        return remote(chip_rows(part, b, first), r1.at[b, 0], rsend.at[b, 1], rrecv.at[b, 1], first)

    def second_copy(b):
        return remote(s2.at[b], r2.at[b], rsend.at[b, 2], rrecv.at[b, 2], second)

    def last_copy(b):
        rows = pl.ds(pl.multiple_of((1 - core) * TOKENS, TOKENS), TOKENS)
        return remote(fin.at[b, rows], r3.at[b], rsend.at[b, 3], rrecv.at[b, 3], flip[1])

    def wide_rows(dev):
        return pl.ds(pl.multiple_of((dev // 2) * 64, 64), 64)

    def fold(b):
        far_copy(b).wait_recv()
        s2[b] = part[b, wide_rows(second), :] + r1[b, 1]
        second_copy(b).start()

    def finish(b):
        near_copy(b).wait_recv()
        second_copy(b).wait_recv()
        fin[b] = part[b, wide_rows(me), :] + r1[b, 0] + r2[b]
        last_copy(b).start()

    def write_out(b, out):
        last_copy(b).wait_recv()
        mine = fin[b, pl.ds(pl.multiple_of(core * TOKENS, TOKENS), TOKENS), :]
        other = r3[b]
        left = jnp.where(core == 0, mine, other)
        right = jnp.where(core == 0, other, mine)
        rows = slice(b * TOKENS, (b + 1) * TOKENS)
        yv[b, :, :HALF] = (hv[rows, :HALF].astype(F32) + left).astype(BF16)
        yv[b, :, HALF:] = (hv[rows, HALF:].astype(F32) + right).astype(BF16)
        copy = local(yv.at[b], out, sem_out.at[b])
        copy.start()
        return copy

    relay(0)
    relay_far(0)
    gathered(0)
    pick(0)
    relay(1)
    experts(0)
    o_copy(0).start()
    relay_far(1)
    o_wait(0)
    combine(0)
    far_copy(0).start()
    near_copy(0).start()
    gathered(1)
    pick(1)
    experts(1)
    o_copy(1).start()
    fold(0)
    o_wait(1)
    combine(1)
    far_copy(1).start()
    near_copy(1).start()
    finish(0)
    fold(1)
    done_a = write_out(0, out_a)
    finish(1)
    done_b = write_out(1, out_b)

    for k in range(1, GROUP):
        meta_copy(k).wait_send()
    for b in range(2):
        for make in (d_near_x, d_near_y, d_sib, d_fwd_x, d_fwd_y, d_sib_x, d_sib_y, d_sib_d, o_copy, far_copy, near_copy, second_copy, last_copy):
            make(b).wait_send()
    done_a.wait()
    done_b.wait()


def solution(mesh):
    row_spec = P(("dp", "ep"), None)
    full_spec = P(None, None, None)
    gain_spec = P(None)
    expert_spec = P("ep", None, None)
    in_specs = (row_spec,) * 8 + (gain_spec,) + (full_spec,) * 4 + (gain_spec,) + (expert_spec,) * 3

    any_spec = pl.BlockSpec(memory_space=pl.ANY)
    VM = pltpu.VMEM
    DMA = pltpu.SemaphoreType.DMA
    scratch = [
        VM((2 * TOKENS, DIM), BF16),
        VM((2, 1, DIM), BF16),
        VM((2, SLOTS, TOKENS), jnp.int32),
        VM((2, SLOTS, TOKENS), jnp.int32),
        VM((2, SLOTS, TOKENS), BF16),
        VM((3, CHUNKS, CHUNK, DIM), BF16),
        VM((DIM, DIM), BF16),
        VM((LOCAL, DIM, FFN), BF16),
        VM((LOCAL, DIM, FFN), BF16),
        VM((LOCAL, FFN, DIM), BF16),
        VM((2 * TOKENS, DIM), BF16),
        VM((3, CHUNKS, 2 * TOKENS, CHUNK), BF16),
        VM((2 * TOKENS, DIM), BF16),
        VM((2 * TOKENS, DIM), BF16),
        VM((2, ROWS, DIM), BF16),
        VM((GROUP, 2, 2, SLOTS, 128), F32),
        VM((2, LROWS, ROWS), BF16),
        VM((2, 2 * LROWS, ROWS), BF16),
        VM((LROWS, DIM), BF16),
        VM((2, 2, 2 * LROWS, HALF), BF16),
        VM((2, ROWS, HALF), F32),
        VM((2, 2, 2 * TOKENS, HALF), F32),
        VM((2, 2 * TOKENS, HALF), F32),
        VM((2, 2 * TOKENS, HALF), F32),
        VM((2, 2 * TOKENS, HALF), F32),
        VM((2, TOKENS, HALF), F32),
        VM((2, TOKENS, DIM), BF16),
        DMA((10,)),
        DMA((3, CHUNKS)),
        DMA,
        DMA((3, LOCAL)),
        DMA((2,)),
        DMA((GROUP,)),
        DMA((GROUP,)),
        DMA((2, 8)),
        DMA((2, 8)),
        DMA((2,)),
        DMA((2,)),
        DMA((2, 4)),
        DMA((2, 4)),
    ]

    def device_fn(tokens_a, experts_a, slots_a, gates_a, tokens_b, experts_b, slots_b, gates_b, attn_gain, w_query, w_key, w_value, w_out, moe_gain, w_gate, w_up, w_down):
        def heads_first(w):
            return jnp.transpose(w, (1, 2, 0)).reshape(DIM, DIM)

        out = jax.ShapeDtypeStruct((TOKENS, DIM), BF16)
        return pl.pallas_call(
            kernel,
            out_shape=(out, out),
            in_specs=[any_spec] * 17,
            out_specs=(any_spec, any_spec),
            scratch_shapes=scratch,
            compiler_params=pltpu.CompilerParams(
                collective_id=0, has_side_effects=True, vmem_limit_bytes=66_000_000,
            ),
            name="moe_layer",
        )(
            tokens_a, experts_a.T, slots_a.T, gates_a.T, tokens_b, experts_b.T, slots_b.T, gates_b.T,
            attn_gain.reshape(1, DIM), heads_first(w_query), heads_first(w_key), heads_first(w_value),
            w_out.reshape(DIM, DIM), moe_gain.reshape(1, DIM), w_gate, w_up, w_down,
        )

    return jax.shard_map(device_fn, mesh=mesh, in_specs=in_specs, out_specs=(row_spec, row_spec), check_vma=False)
```

time: 110 us -> 61.1 us (0.56)
  Pallas kernels: 0 us -> 54.6 us
  matrix products: 51.6 us -> 0 us
  waiting for transfers between devices: 26.1 us -> 0 us
  starting transfers between devices: 11.2 us -> 0 us
  local copies, waits for them, and re-layouts: 12.8 us -> 5.65 us
  other arithmetic: 6.47 us -> 0 us
    pallas_call x0 -> x1, Pallas kernels: none -> 54.6 us  [device_fn(): pl.pallas_call(kernel, out_shape=(out, out), in_specs=[any_spec] * 17, ou...]
    dot_general x16 -> x0, matrix products: 51.6 us -> none  [the longest x2 9.71 us: expert_ffn(): jnp.einsum('pecd,edf->pecf', received, w_gate, preferred_element_type=jnp...]
    all_to_all x4 -> x0, waiting for transfers between devices: 26.1 us -> none  [the longest x2 14.3 us: moe_layer(): returned = lax.all_to_all(expert_out, 'ep', 0, 0, tiled=True)]
    all_to_all x4 -> x0, starting transfers between devices: 11.2 us -> none  [the longest x2 6.6 us: moe_layer(): lax.all_to_all(dispatched, 'ep', 0, 0, tiled=True)]
    gather x4 -> x0, local copies, waits for them, and re-layouts: 6.97 us -> none  [the longest x2 4.45 us: dispatch_rows(): jnp.take(normed, source, axis=0, mode='fill', fill_value=0)]
    scatter x2 -> x0, local copies, waits for them, and re-layouts: 2.79 us -> none  [dispatch_rows(): jnp.full((experts_total * capacity,), seq_len, jnp.int32).at[dest_row]]
    unnamed x34 -> x2, local copies, waits for them, and re-layouts: 0.29 us -> 3.08 us
    convert_element_type x5 -> x0, other arithmetic: 2.28 us -> none  [the longest x2 1.33 us: combine_rows(): return (residual.astype(jnp.float32) + mixed_sum).astype(jnp.bfloat16)]
  transfers between devices with their start and end apart: 4 -> 0, of which waited for: 4 -> 0; matrix products, arithmetic and copies ran while one was open for 29% -> 0% of each run, Pallas kernels for 0% -> 0%
where the time goes in v1:
time: 61.1 us; the launch traced here: 60.9 us
  Pallas kernels  54.6 us (89%)
  local copies, waits for them, and re-layouts  5.65 us (9%)
  between operations  0.64 us (1%)
    pallas_call x1, Pallas kernels, device_fn(): pl.pallas_call(kernel, out_shape=(out, out), in_specs=[any_spec] * 17, ou...  54.6 us
    unnamed x2, local copies, waits for them, and re-layouts  3.08 us
    reshape x1, local copies, waits for them, and re-layouts, device_fn(): attn_gain.reshape(1, DIM)  1.29 us
    reshape x1, local copies, waits for them, and re-layouts, device_fn(): moe_gain.reshape(1, DIM)  1.28 us

profile of v1, /device:TPU:0, one launch (start us, length us, event | category | flops | bytes accessed | tf_op | source)
XLA Modules:
  0.0 60.9 jit_solution(14231172274810326549)
XLA Ops:
  0.6 1.3 %reshape.22.again_hbm = bf16[1,1536]{1,0:T(2,128)(2,1)} reshape(bf16[1536]{0:T(1024)(128)(2,1)} %param.25) | data formatting | bytes 6144 | tf_op jit(solution)/shard_map/reshape | solution.py:472
  1.9 1.3 %reshape.27.mgain_hbm = bf16[1,1536]{1,0:T(2,128)(2,1)} reshape(bf16[1536]{0:T(1024)(128)(2,1)} %param.30) | data formatting | bytes 6144 | tf_op jit(solution)/shard_map/reshape | solution.py:473
  3.2 54.6 %moe_layer.1 = (bf16[32,1536]{1,0:T(8,128)(2,1)}, bf16[32,1536]{1,0:T(8,128)(2,1)}) custom-call(bf16[32,1536]{1,0:T(8,128)(2,1)} %tok_a.1, s32[8,32]{1,0:T(8,128)} %bitcast.20, s32[8,32]{1,0:T(8,128)} %bitcast.21, bf16[8,32]{1,0:T(8,128)(2,1)} %bitcast.24, bf16[32,1536]{1,0:T(8,128)(2,1)} %tok_b.1, s32[8,32]{1,0:T(8,128)} %bitcast.22, s32[8,32]{1,0:T(8,128)} %bitcast.23, ...), custom_call_target="tpu_custom_call" | custom-call | tf_op jit(solution)/shard_map/moe_layer/pallas_call | solution.py:460
  57.8 1.5 %copy.21 = bf16[32,1536]{1,0:T(8,128)(2,1)} copy(bf16[32,1536]{1,0:T(8,128)(2,1)} %get-tuple-element.4) | data formatting | bytes 196608
  59.4 1.5 %copy.22 = bf16[32,1536]{1,0:T(8,128)(2,1)} copy(bf16[32,1536]{1,0:T(8,128)(2,1)} %get-tuple-element.5) | data formatting | bytes 196608

commit v2 on v1

--- a/solution.py
+++ b/solution.py
@@ -93,18 +93,26 @@
         rows = pl.ds(pl.multiple_of(c * CHUNK, CHUNK), CHUNK)
         return local(whbm[which].at[rows], wqkv.at[which, c], sem_qkv.at[which, c])
 
-    for c in range(CHUNKS):
-        for which in range(3):
-            qkv_copy(which, c).start()
+    for which in range(3):
+        qkv_copy(which, 0).start()
     wo_copy = local(wo_hbm, wov, sem_o)
-    wo_copy.start()
 
     barrier = pltpu.get_barrier_semaphore()
     for k in range(1, GROUP):
         pl.semaphore_signal(barrier, inc=1, device_id={"ep": flip[k]}, device_id_type=MESH)
 
-    for copy in small[:6]:
+    for copy in small:
         copy.wait()
+    for c in range(1, CHUNKS):
+        for which in range(3):
+            qkv_copy(which, c).start()
+    wo_copy.start()
+
+    def gain_row(i):
+        g = gains[i].astype(F32)
+        return jnp.concatenate([g[j:j + 1] for j in range(DIM // 128)], axis=1)
+
+    norm_a[...] = rms_rows(xv[...].astype(F32), gain_row(0))
 
     lane = lax.broadcasted_iota(jnp.int32, (SLOTS, 128), 1)
     my_lanes = lane // TOKENS == me % 4
@@ -123,19 +131,65 @@
     for k in range(1, GROUP):
         meta_copy(k).start()
 
-    for copy in small[6:]:
-        copy.wait()
-    norm_a[...] = rms_rows(xv[...].astype(F32), gains[0].astype(F32))
-
-    def qkv_step(c, carry):
+
+    n2 = 2 * TOKENS
+    lane128 = lax.broadcasted_iota(jnp.int32, (n2, 128), 1)
+    row128 = lax.broadcasted_iota(jnp.int32, (n2, 128), 0)
+    key = lane128 % n2
+    visible = (key // TOKENS == row128 // TOKENS) & (key <= row128)
+    low = lane128 < n2
+    head_of = lax.broadcasted_iota(jnp.int32, (n2, CHUNK), 1) // n2
+    scale = 64.0 ** -0.5
+
+    def spread(x):
+        zero = jnp.zeros_like(x)
+        return jnp.concatenate([jnp.where(head_of == g, x, zero) for g in range(CHUNK // n2)], axis=0)
+
+    def softmax_pair(s):
+        s = jnp.where(visible, s * scale, MASK_VALUE)
+        m0 = jnp.max(jnp.where(low, s, -jnp.inf), axis=-1, keepdims=True)
+        m1 = jnp.max(jnp.where(low, -jnp.inf, s), axis=-1, keepdims=True)
+        p = jnp.exp(s - jnp.where(low, m0, m1))
+        d0 = jnp.sum(jnp.where(low, p, 0.0), axis=-1, keepdims=True)
+        d1 = jnp.sum(jnp.where(low, 0.0, p), axis=-1, keepdims=True)
+        return (p / jnp.where(low, d0, d1)).astype(BF16)
+
+    def project(which, c):
+        prod = lax.dot_general(norm_a[...], wqkv[which, c], NT, preferred_element_type=F32)
+        return prod.astype(BF16)
+
+    def scores(c):
+        return lax.dot_general(qkv[0, c], spread(qkv[1, c]), NT, preferred_element_type=F32)
+
+    def softmax(s):
+        return jnp.concatenate([softmax_pair(s[:, i * 128:(i + 1) * 128]) for i in range(CHUNK // 128)], axis=1)
+
+    def store_context(c, p, values):
+        ctx[:, pl.ds(pl.multiple_of(c * CHUNK, CHUNK), CHUNK)] = jnp.dot(p, values, preferred_element_type=F32).astype(BF16)
+
+    def wait_chunk(c):
         for which in range(3):
             qkv_copy(which, c).wait()
-        for which in range(3):
-            prod = lax.dot_general(norm_a[...], wqkv[which, c], NT, preferred_element_type=F32)
-            qkv[which, c] = prod.astype(BF16)
+
+    wait_chunk(0)
+    for which in range(3):
+        qkv[which, 0] = project(which, 0)
+
+    def qkv_step(c, carry):
+        wait_chunk(c)
+        values = spread(qkv[2, c - 1])
+        s = scores(c - 1)
+        q = project(0, c)
+        p = softmax(s)
+        k = project(1, c)
+        store_context(c - 1, p, values)
+        v = project(2, c)
+        qkv[0, c] = q
+        qkv[1, c] = k
+        qkv[2, c] = v
         return carry
 
-    lax.fori_loop(0, CHUNKS, qkv_step, 0)
+    lax.fori_loop(1, CHUNKS, qkv_step, 0)
 
     def expert_copies(e):
         return (
@@ -148,36 +202,13 @@
         for copy in expert_copies(e):
             copy.start()
 
-    n2 = 2 * TOKENS
-    lane128 = lax.broadcasted_iota(jnp.int32, (n2, 128), 1)
-    row128 = lax.broadcasted_iota(jnp.int32, (n2, 128), 0)
-    key = lane128 % n2
-    visible = (key // TOKENS == row128 // TOKENS) & (key <= row128)
-    low = lane128 < n2
-    scale = 64.0 ** -0.5
-    for pair in range(DIM // 128):
-        c, off = pair // 2, (pair % 2) * 128
-        q = qkv[0, c, :, off:off + 128]
-        k = qkv[1, c, :, off:off + 128]
-        v = qkv[2, c, :, off:off + 128]
-        zero = jnp.zeros_like(k)
-        kk = jnp.concatenate([jnp.where(low, k, zero), jnp.where(low, zero, k)], axis=0)
-        vv = jnp.concatenate([jnp.where(low, v, zero), jnp.where(low, zero, v)], axis=0)
-        s = lax.dot_general(q, kk, NT, preferred_element_type=F32) * scale
-        s = jnp.where(visible, s, MASK_VALUE)
-        m0 = jnp.max(jnp.where(low, s, -jnp.inf), axis=-1, keepdims=True)
-        m1 = jnp.max(jnp.where(low, -jnp.inf, s), axis=-1, keepdims=True)
-        p = jnp.exp(s - jnp.where(low, m0, m1))
-        d0 = jnp.sum(jnp.where(low, p, 0.0), axis=-1, keepdims=True)
-        d1 = jnp.sum(jnp.where(low, 0.0, p), axis=-1, keepdims=True)
-        p = (p / jnp.where(low, d0, d1)).astype(BF16)
-        ctx[:, pair * 128:(pair + 1) * 128] = jnp.dot(p, vv, preferred_element_type=F32).astype(BF16)
+    store_context(CHUNKS - 1, softmax(scores(CHUNKS - 1)), spread(qkv[2, CHUNKS - 1]))
 
     wo_copy.wait()
     attn = jnp.dot(ctx[...], wov[...], preferred_element_type=F32)
     h = (xv[...].astype(F32) + attn).astype(BF16)
     hv[...] = h
-    u = rms_rows(h.astype(F32), gains[1].astype(F32))
+    u = rms_rows(h.astype(F32), gain_row(1))
     my_rows = pl.ds(pl.multiple_of(me * TOKENS, TOKENS), TOKENS)
     uall[0, my_rows, :] = u[:TOKENS]
     uall[1, my_rows, :] = u[TOKENS:]
@@ -282,38 +313,43 @@
         d_wait(b, 7, flip[7])
 
     def pick(b):
-        def pick_step(n, carry):
-            cols = pl.ds(pl.multiple_of(n * CHUNK, CHUNK), CHUNK)
+        for n in range(CHUNKS):
+            cols = slice(n * CHUNK, (n + 1) * CHUNK)
             picked[:, cols] = jnp.dot(disp[b], uall[b, :, cols], preferred_element_type=F32).astype(BF16)
-            return carry
-
-        lax.fori_loop(0, CHUNKS, pick_step, 0)
+
+    def o_copy(b, e):
+        src = o2.at[b, 1 - core, pl.ds(e * 64, 64)]
+        dst = o2.at[b, 1 - core, pl.ds(LROWS + e * 64, 64)]
+        return remote(src, dst, osend.at[b, e], orecv.at[b, e], flip[1])
+
+    def o_wait(b):
+        for e in range(LOCAL):
+            ref = o2.at[b, core, pl.ds(LROWS + e * 64, 64)]
+            remote(ref, ref, osend.at[b, e], orecv.at[b, e], flip[1]).wait_recv()
+
+    def gate_up(e):
+        x = picked[e * 64:(e + 1) * 64, :]
+        g = jnp.dot(x, wgv[e], preferred_element_type=F32)
+        up = jnp.dot(x, wuv[e], preferred_element_type=F32)
+        return g, up
 
     def experts(b):
-        def expert_step(e, carry):
-            if b == 0:
+        if b == 0:
+            for e in range(LOCAL):
                 for copy in expert_copies(e):
                     copy.wait()
-            rows = pl.ds(pl.multiple_of(e * 64, 64), 64)
-            x = picked[rows, :]
-            g = jnp.dot(x, wgv[e], preferred_element_type=F32)
-            up = jnp.dot(x, wuv[e], preferred_element_type=F32)
+        g, up = gate_up(0)
+        for e in range(LOCAL):
             hidden = (g * (1.0 / (1.0 + jnp.exp(-g))) * up).astype(BF16)
+            if e + 1 < LOCAL:
+                g, up = gate_up(e + 1)
             o = jnp.dot(hidden, wdv[e], preferred_element_type=F32).astype(BF16)
+            rows = slice(e * 64, (e + 1) * 64)
             o2[b, 0, rows, :] = o[:, :HALF]
             o2[b, 1, rows, :] = o[:, HALF:]
-            return carry
-
-        lax.fori_loop(0, LOCAL, expert_step, 0)
-
-    def o_copy(b):
-        src = o2.at[b, 1 - core, pl.ds(0, LROWS)]
-        dst = o2.at[b, 1 - core, pl.ds(LROWS, LROWS)]
-        return remote(src, dst, osend.at[b], orecv.at[b], flip[1])
-
-    def o_wait(b):
-        ref = o2.at[b, core, pl.ds(LROWS, LROWS)]
-        remote(ref, ref, osend.at[b], orecv.at[b], flip[1]).wait_recv()
+            if e > 0:
+                o_copy(b, e - 1).start()
+        o_copy(b, LOCAL - 1).start()
 
     def combine(b):
         for n in range(HALF // CHUNK):
@@ -369,7 +405,6 @@
     pick(0)
     relay(1)
     experts(0)
-    o_copy(0).start()
     relay_far(1)
     o_wait(0)
     combine(0)
@@ -378,7 +413,6 @@
     gathered(1)
     pick(1)
     experts(1)
-    o_copy(1).start()
     fold(0)
     o_wait(1)
     combine(1)
@@ -393,8 +427,10 @@
     for k in range(1, GROUP):
         meta_copy(k).wait_send()
     for b in range(2):
-        for make in (d_near_x, d_near_y, d_sib, d_fwd_x, d_fwd_y, d_sib_x, d_sib_y, d_sib_d, o_copy, far_copy, near_copy, second_copy, last_copy):
+        for make in (d_near_x, d_near_y, d_sib, d_fwd_x, d_fwd_y, d_sib_x, d_sib_y, d_sib_d, far_copy, near_copy, second_copy, last_copy):
             make(b).wait_send()
+        for e in range(LOCAL):
+            o_copy(b, e).wait_send()
     done_a.wait()
     done_b.wait()
 
@@ -411,7 +447,7 @@
     DMA = pltpu.SemaphoreType.DMA
     scratch = [
         VM((2 * TOKENS, DIM), BF16),
-        VM((2, 1, DIM), BF16),
+        VM((2, DIM // 128, 128), BF16),
         VM((2, SLOTS, TOKENS), jnp.int32),
         VM((2, SLOTS, TOKENS), jnp.int32),
         VM((2, SLOTS, TOKENS), BF16),
@@ -446,8 +482,8 @@
         DMA((GROUP,)),
         DMA((2, 8)),
         DMA((2, 8)),
-        DMA((2,)),
-        DMA((2,)),
+        DMA((2, LOCAL)),
+        DMA((2, LOCAL)),
         DMA((2, 4)),
         DMA((2, 4)),
     ]
@@ -469,8 +505,8 @@
             name="moe_layer",
         )(
             tokens_a, experts_a.T, slots_a.T, gates_a.T, tokens_b, experts_b.T, slots_b.T, gates_b.T,
-            attn_gain.reshape(1, DIM), heads_first(w_query), heads_first(w_key), heads_first(w_value),
-            w_out.reshape(DIM, DIM), moe_gain.reshape(1, DIM), w_gate, w_up, w_down,
+            attn_gain.reshape(DIM // 128, 128), heads_first(w_query), heads_first(w_key), heads_first(w_value),
+            w_out.reshape(DIM, DIM), moe_gain.reshape(DIM // 128, 128), w_gate, w_up, w_down,
         )
 
     return jax.shard_map(device_fn, mesh=mesh, in_specs=in_specs, out_specs=(row_spec, row_spec), check_vma=False)

time: 61.1 us -> 50.6 us (0.83)
  Pallas kernels: 54.6 us -> 46.7 us
  local copies, waits for them, and re-layouts: 5.65 us -> 3.08 us
    pallas_call x1, Pallas kernels: 54.6 us -> 46.7 us  [device_fn(): pl.pallas_call(kernel, out_shape=(out, out), in_specs=[any_spec] * 17, ou...]
    reshape x2 -> x0, local copies, waits for them, and re-layouts: 2.57 us -> none  [the longest x1 1.29 us: device_fn(): attn_gain.reshape(1, DIM)]
where the time goes in v2:
time: 50.6 us; the launch traced here: 50.4 us
  Pallas kernels  46.7 us (92%)
  local copies, waits for them, and re-layouts  3.08 us (6%)
  between operations  0.65 us (1%)
    pallas_call x1, Pallas kernels, device_fn(): pl.pallas_call(kernel, out_shape=(out, out), in_specs=[any_spec] * 17, ou...  46.7 us
    unnamed x2, local copies, waits for them, and re-layouts  3.08 us

profile of v2, /device:TPU:0, one launch (start us, length us, event | category | flops | bytes accessed | tf_op | source)
XLA Modules:
  0.0 50.4 jit_solution(3077740962309935056)
XLA Ops:
  0.6 46.7 %moe_layer.1 = (bf16[32,1536]{1,0:T(8,128)(2,1)}, bf16[32,1536]{1,0:T(8,128)(2,1)}) custom-call(bf16[32,1536]{1,0:T(8,128)(2,1)} %tok_a.1, s32[8,32]{1,0:T(8,128)} %bitcast.22, s32[8,32]{1,0:T(8,128)} %bitcast.23, bf16[8,32]{1,0:T(8,128)(2,1)} %bitcast.28, bf16[32,1536]{1,0:T(8,128)(2,1)} %tok_b.1, s32[8,32]{1,0:T(8,128)} %bitcast.24, s32[8,32]{1,0:T(8,128)} %bitcast.25, ...), custom_call_target="tpu_custom_call" | custom-call | tf_op jit(solution)/shard_map/moe_layer/pallas_call | solution.py:496
  47.3 1.5 %copy.21 = bf16[32,1536]{1,0:T(8,128)(2,1)} copy(bf16[32,1536]{1,0:T(8,128)(2,1)} %get-tuple-element.4) | data formatting | bytes 196608
  48.9 1.5 %copy.22 = bf16[32,1536]{1,0:T(8,128)(2,1)} copy(bf16[32,1536]{1,0:T(8,128)(2,1)} %get-tuple-element.5) | data formatting | bytes 196608

commit v3 on v2

--- a/solution.py
+++ b/solution.py
@@ -20,6 +20,7 @@
 HALF = DIM // 2
 CHUNK = 256
 CHUNKS = DIM // CHUNK
+BLOCKS = ((0, 1), (1, 2), (2, 4), (4, 6))
 ROWS = GROUP * TOKENS
 LROWS = LOCAL * GROUP * SLOTS
 F32 = jnp.float32
@@ -29,6 +30,10 @@
 TN = (((0,), (0,)), ((), ()))
 
 
+def twice(x):
+    return jnp.concatenate([x, x], axis=0)
+
+
 def rms_rows(rows_f, gain):
     inv = lax.rsqrt(jnp.mean(rows_f * rows_f, axis=-1, keepdims=True) + NORM_EPS)
     return (rows_f * inv * gain).astype(BF16)
@@ -37,11 +42,11 @@
 def kernel(
     tok_a, exp_a, slot_a, gate_a, tok_b, exp_b, slot_b, gate_b,
     again_hbm, wq_hbm, wk_hbm, wv_hbm, wo_hbm, mgain_hbm, wg_hbm, wu_hbm, wd_hbm,
-    out_a, out_b,
+    out_y,
     xv, gains, ev, sv, gv,
     wqkv, wov, wgv, wuv, wdv,
-    norm_a, qkv, ctx, hv, uall, meta, disp, comb, picked, o2, part, r1, s2, r2, fin, r3, yv,
-    sem_in, sem_qkv, sem_o, sem_exp, sem_out,
+    norm_a, qkv, ctx, hv, uall, meta, disp, comb, picked, o2, part, r1, s2, r2, fin, r3,
+    sem_in, sem_qkv, sem_o, sem_exp,
     msend, mrecv, dsend, drecv, osend, orecv, rsend, rrecv,
 ):
     me = lax.axis_index("ep")
@@ -91,7 +96,7 @@
 
     def qkv_copy(which, c):
         rows = pl.ds(pl.multiple_of(c * CHUNK, CHUNK), CHUNK)
-        return local(whbm[which].at[rows], wqkv.at[which, c], sem_qkv.at[which, c])
+        return local(whbm[which].at[rows], wqkv.at[which, rows], sem_qkv.at[which, c])
 
     for which in range(3):
         qkv_copy(which, 0).start()
@@ -141,10 +146,6 @@
     head_of = lax.broadcasted_iota(jnp.int32, (n2, CHUNK), 1) // n2
     scale = 64.0 ** -0.5
 
-    def spread(x):
-        zero = jnp.zeros_like(x)
-        return jnp.concatenate([jnp.where(head_of == g, x, zero) for g in range(CHUNK // n2)], axis=0)
-
     def softmax_pair(s):
         s = jnp.where(visible, s * scale, MASK_VALUE)
         m0 = jnp.max(jnp.where(low, s, -jnp.inf), axis=-1, keepdims=True)
@@ -154,42 +155,40 @@
         d1 = jnp.sum(jnp.where(low, 0.0, p), axis=-1, keepdims=True)
         return (p / jnp.where(low, d0, d1)).astype(BF16)
 
-    def project(which, c):
-        prod = lax.dot_general(norm_a[...], wqkv[which, c], NT, preferred_element_type=F32)
-        return prod.astype(BF16)
+    def spread(x):
+        zero = jnp.zeros_like(x)
+        return jnp.concatenate([jnp.where(head_of == g, x, zero) for g in range(CHUNK // n2)], axis=0)
+
+    def lanes(which, c):
+        return qkv[which, :, c * CHUNK:(c + 1) * CHUNK]
+
+    def project(which, lo, hi):
+        cols = slice(lo * CHUNK, hi * CHUNK)
+        prod = lax.dot_general(norm_a[...], wqkv[which, cols, :], NT, preferred_element_type=F32)
+        qkv[which, :, cols] = prod.astype(BF16)
 
     def scores(c):
-        return lax.dot_general(qkv[0, c], spread(qkv[1, c]), NT, preferred_element_type=F32)
+        return lax.dot_general(lanes(0, c), spread(lanes(1, c)), NT, preferred_element_type=F32)
 
     def softmax(s):
         return jnp.concatenate([softmax_pair(s[:, i * 128:(i + 1) * 128]) for i in range(CHUNK // 128)], axis=1)
 
-    def store_context(c, p, values):
-        ctx[:, pl.ds(pl.multiple_of(c * CHUNK, CHUNK), CHUNK)] = jnp.dot(p, values, preferred_element_type=F32).astype(BF16)
-
-    def wait_chunk(c):
-        for which in range(3):
-            qkv_copy(which, c).wait()
-
-    wait_chunk(0)
-    for which in range(3):
-        qkv[which, 0] = project(which, 0)
-
-    def qkv_step(c, carry):
-        wait_chunk(c)
-        values = spread(qkv[2, c - 1])
-        s = scores(c - 1)
-        q = project(0, c)
-        p = softmax(s)
-        k = project(1, c)
-        store_context(c - 1, p, values)
-        v = project(2, c)
-        qkv[0, c] = q
-        qkv[1, c] = k
-        qkv[2, c] = v
-        return carry
-
-    lax.fori_loop(1, CHUNKS, qkv_step, 0)
+    def store_context(c, p):
+        ctx[:, c * CHUNK:(c + 1) * CHUNK] = jnp.dot(p, spread(lanes(2, c)), preferred_element_type=F32).astype(BF16)
+
+    before = ()
+    for lo, hi in BLOCKS:
+        for c in range(lo, hi):
+            for which in range(3):
+                qkv_copy(which, c).wait()
+        raw = [scores(c) for c in before]
+        project(0, lo, hi)
+        probs = [softmax(s) for s in raw]
+        project(1, lo, hi)
+        for c, p in zip(before, probs):
+            store_context(c, p)
+        project(2, lo, hi)
+        before = tuple(range(lo, hi))
 
     def expert_copies(e):
         return (
@@ -202,10 +201,13 @@
         for copy in expert_copies(e):
             copy.start()
 
-    store_context(CHUNKS - 1, softmax(scores(CHUNKS - 1)), spread(qkv[2, CHUNKS - 1]))
+    raw = [scores(c) for c in before]
+    probs = [softmax(s) for s in raw]
+    for c, p in zip(before, probs):
+        store_context(c, p)
 
     wo_copy.wait()
-    attn = jnp.dot(ctx[...], wov[...], preferred_element_type=F32)
+    attn = jnp.dot(twice(ctx[...]), wov[...], preferred_element_type=F32)[:n2]
     h = (xv[...].astype(F32) + attn).astype(BF16)
     hv[...] = h
     u = rms_rows(h.astype(F32), gain_row(1))
@@ -222,38 +224,42 @@
 
     H = TOKENS // 2
 
-    def d_near_x(b):
-        return disp_copy(b, 0, me, flip[2], 2)
-
-    def d_near_y(b):
-        return disp_copy(b, 1, me, flip[4], 4)
+    def d_x(b, part):
+        return disp_copy(b, part, me, flip[2], part, part * H, H)
+
+    def d_y(b, part):
+        return disp_copy(b, 2 + part, me, flip[4], 2 + part, part * H, H)
 
     def d_sib(b):
-        return disp_copy(b, 2, me, flip[1], 1)
+        return disp_copy(b, 6, me, flip[1], 6)
 
     def d_fwd_x(b):
-        return disp_copy(b, 3, flip[2], flip[4], 6, 0, H)
+        return disp_copy(b, 4, flip[2], flip[4], 4, 0, H)
 
     def d_fwd_y(b):
-        return disp_copy(b, 4, flip[4], flip[2], 0, H, H)
+        return disp_copy(b, 5, flip[4], flip[2], 5, H, H)
 
     def d_sib_x(b):
-        return disp_copy(b, 5, flip[2], flip[1], 3)
+        return disp_copy(b, 7, flip[2], flip[1], 7)
 
     def d_sib_y(b):
-        return disp_copy(b, 6, flip[4], flip[1], 5)
+        return disp_copy(b, 8, flip[4], flip[1], 8)
 
     def d_sib_d(b):
-        return disp_copy(b, 7, flip[6], flip[1], 7)
+        return disp_copy(b, 9, flip[6], flip[1], 9)
 
     def d_wait(b, slot, dev, lo=0, n=TOKENS):
         ref = block(b, dev, lo, n)
         remote(ref, ref, dsend.at[b, 0], drecv.at[b, slot], flip[1]).wait_recv()
 
-    for b in range(2):
-        d_near_x(b).start()
-        d_near_y(b).start()
+    def send_own(b):
+        d_x(b, 0).start()
+        d_y(b, 1).start()
+        d_x(b, 1).start()
+        d_y(b, 0).start()
         d_sib(b).start()
+
+    send_own(0)
 
     for k in range(1, GROUP):
         remote(meta.at[flip[k]], meta.at[flip[k]], msend.at[k], mrecv.at[k], flip[k]).wait_recv()
@@ -294,23 +300,27 @@
                     disp[b, e * 64:(e + 1) * 64, :] = jnp.where(owner_hit, wide, 0.0).astype(BF16)
 
     def relay(b):
-        d_wait(b, 2, flip[2])
+        d_wait(b, 0, flip[2], 0, H)
         d_fwd_x(b).start()
+        d_wait(b, 3, flip[4], H, H)
+        d_fwd_y(b).start()
+
+    def relay_near(b):
+        d_wait(b, 1, flip[2], H, H)
         d_sib_x(b).start()
-        d_wait(b, 4, flip[4])
-        d_fwd_y(b).start()
+        d_wait(b, 2, flip[4], 0, H)
         d_sib_y(b).start()
 
     def relay_far(b):
-        d_wait(b, 6, flip[6], 0, H)
-        d_wait(b, 0, flip[6], H, H)
+        d_wait(b, 4, flip[6], 0, H)
+        d_wait(b, 5, flip[6], H, H)
         d_sib_d(b).start()
 
     def gathered(b):
-        d_wait(b, 1, flip[1])
-        d_wait(b, 3, flip[3])
-        d_wait(b, 5, flip[5])
-        d_wait(b, 7, flip[7])
+        d_wait(b, 6, flip[1])
+        d_wait(b, 7, flip[3])
+        d_wait(b, 8, flip[5])
+        d_wait(b, 9, flip[7])
 
     def pick(b):
         for n in range(CHUNKS):
@@ -328,10 +338,10 @@
             remote(ref, ref, osend.at[b, e], orecv.at[b, e], flip[1]).wait_recv()
 
     def gate_up(e):
-        x = picked[e * 64:(e + 1) * 64, :]
+        x = twice(picked[e * 64:(e + 1) * 64, :])
         g = jnp.dot(x, wgv[e], preferred_element_type=F32)
         up = jnp.dot(x, wuv[e], preferred_element_type=F32)
-        return g, up
+        return g[:64], up[:64]
 
     def experts(b):
         if b == 0:
@@ -343,7 +353,7 @@
             hidden = (g * (1.0 / (1.0 + jnp.exp(-g))) * up).astype(BF16)
             if e + 1 < LOCAL:
                 g, up = gate_up(e + 1)
-            o = jnp.dot(hidden, wdv[e], preferred_element_type=F32).astype(BF16)
+            o = jnp.dot(twice(hidden), wdv[e], preferred_element_type=F32)[:64].astype(BF16)
             rows = slice(e * 64, (e + 1) * 64)
             o2[b, 0, rows, :] = o[:, :HALF]
             o2[b, 1, rows, :] = o[:, HALF:]
@@ -393,17 +403,17 @@
         left = jnp.where(core == 0, mine, other)
         right = jnp.where(core == 0, other, mine)
         rows = slice(b * TOKENS, (b + 1) * TOKENS)
-        yv[b, :, :HALF] = (hv[rows, :HALF].astype(F32) + left).astype(BF16)
-        yv[b, :, HALF:] = (hv[rows, HALF:].astype(F32) + right).astype(BF16)
-        copy = local(yv.at[b], out, sem_out.at[b])
-        copy.start()
-        return copy
+        out[:, :HALF] = (hv[rows, :HALF].astype(F32) + left).astype(BF16)
+        out[:, HALF:] = (hv[rows, HALF:].astype(F32) + right).astype(BF16)
 
     relay(0)
+    send_own(1)
+    relay_near(0)
     relay_far(0)
     gathered(0)
     pick(0)
     relay(1)
+    relay_near(1)
     experts(0)
     relay_far(1)
     o_wait(0)
@@ -420,19 +430,20 @@
     near_copy(1).start()
     finish(0)
     fold(1)
-    done_a = write_out(0, out_a)
+    write_out(0, out_y.at[0])
     finish(1)
-    done_b = write_out(1, out_b)
+    write_out(1, out_y.at[1])
 
     for k in range(1, GROUP):
         meta_copy(k).wait_send()
     for b in range(2):
-        for make in (d_near_x, d_near_y, d_sib, d_fwd_x, d_fwd_y, d_sib_x, d_sib_y, d_sib_d, far_copy, near_copy, second_copy, last_copy):
+        for part_id in range(2):
+            d_x(b, part_id).wait_send()
+            d_y(b, part_id).wait_send()
+        for make in (d_sib, d_fwd_x, d_fwd_y, d_sib_x, d_sib_y, d_sib_d, far_copy, near_copy, second_copy, last_copy):
             make(b).wait_send()
         for e in range(LOCAL):
             o_copy(b, e).wait_send()
-    done_a.wait()
-    done_b.wait()
 
 
 def solution(mesh):
@@ -442,7 +453,7 @@
     expert_spec = P("ep", None, None)
     in_specs = (row_spec,) * 8 + (gain_spec,) + (full_spec,) * 4 + (gain_spec,) + (expert_spec,) * 3
 
-    any_spec = pl.BlockSpec(memory_space=pl.ANY)
+    hbm_spec = pl.BlockSpec(memory_space=pltpu.HBM)
     VM = pltpu.VMEM
     DMA = pltpu.SemaphoreType.DMA
     scratch = [
@@ -451,13 +462,13 @@
         VM((2, SLOTS, TOKENS), jnp.int32),
         VM((2, SLOTS, TOKENS), jnp.int32),
         VM((2, SLOTS, TOKENS), BF16),
-        VM((3, CHUNKS, CHUNK, DIM), BF16),
+        VM((3, DIM, DIM), BF16),
         VM((DIM, DIM), BF16),
         VM((LOCAL, DIM, FFN), BF16),
         VM((LOCAL, DIM, FFN), BF16),
         VM((LOCAL, FFN, DIM), BF16),
         VM((2 * TOKENS, DIM), BF16),
-        VM((3, CHUNKS, 2 * TOKENS, CHUNK), BF16),
+        VM((3, 2 * TOKENS, DIM), BF16),
         VM((2 * TOKENS, DIM), BF16),
         VM((2 * TOKENS, DIM), BF16),
         VM((2, ROWS, DIM), BF16),
@@ -472,16 +483,14 @@
         VM((2, 2 * TOKENS, HALF), F32),
         VM((2, 2 * TOKENS, HALF), F32),
         VM((2, TOKENS, HALF), F32),
-        VM((2, TOKENS, DIM), BF16),
         DMA((10,)),
         DMA((3, CHUNKS)),
         DMA,
         DMA((3, LOCAL)),
-        DMA((2,)),
         DMA((GROUP,)),
         DMA((GROUP,)),
-        DMA((2, 8)),
-        DMA((2, 8)),
+        DMA((2, 10)),
+        DMA((2, 10)),
         DMA((2, LOCAL)),
         DMA((2, LOCAL)),
         DMA((2, 4)),
@@ -492,15 +501,15 @@
         def heads_first(w):
             return jnp.transpose(w, (1, 2, 0)).reshape(DIM, DIM)
 
-        out = jax.ShapeDtypeStruct((TOKENS, DIM), BF16)
-        return pl.pallas_call(
+        out = VM((2, TOKENS, DIM), BF16)
+        y = pl.pallas_call(
             kernel,
-            out_shape=(out, out),
-            in_specs=[any_spec] * 17,
-            out_specs=(any_spec, any_spec),
+            out_shape=out,
+            in_specs=[hbm_spec] * 17,
+            out_specs=pl.BlockSpec(memory_space=pltpu.VMEM),
             scratch_shapes=scratch,
             compiler_params=pltpu.CompilerParams(
-                collective_id=0, has_side_effects=True, vmem_limit_bytes=66_000_000,
+                collective_id=0, has_side_effects=True, vmem_limit_bytes=58000000,
             ),
             name="moe_layer",
         )(
@@ -508,5 +517,6 @@
             attn_gain.reshape(DIM // 128, 128), heads_first(w_query), heads_first(w_key), heads_first(w_value),
             w_out.reshape(DIM, DIM), moe_gain.reshape(DIM // 128, 128), w_gate, w_up, w_down,
         )
+        return y[0], y[1]
 
     return jax.shard_map(device_fn, mesh=mesh, in_specs=in_specs, out_specs=(row_spec, row_spec), check_vma=False)

time: 50.6 us -> 44.6 us (0.88)
  Pallas kernels: 46.7 us -> 43.2 us
  local copies, waits for them, and re-layouts: 3.08 us -> 0.69 us
    pallas_call x1, Pallas kernels: 46.7 us -> 43.2 us  [device_fn(): pl.pallas_call(kernel, out_shape=out, in_specs=[hbm_spec] * 17, out_specs...]
    unnamed x2 -> x0, local copies, waits for them, and re-layouts: 3.08 us -> none
    squeeze x0 -> x1, local copies, waits for them, and re-layouts: none -> 0.69 us  [device_fn(): return (y[0], y[1])]
where the time goes in v3:
time: 44.6 us; the launch traced here: 44.5 us
  Pallas kernels  43.2 us (97%)
  local copies, waits for them, and re-layouts  0.69 us (2%)
  between operations  0.65 us (1%)
    pallas_call x1, Pallas kernels, device_fn(): pl.pallas_call(kernel, out_shape=out, in_specs=[hbm_spec] * 17, out_specs...  43.2 us

profile of v3, /device:TPU:0, one launch (start us, length us, event | category | flops | bytes accessed | tf_op | source)
XLA Modules:
  0.0 44.5 jit_solution(6354466996836805079)
XLA Ops:
  0.6 43.2 %moe_layer.1 = bf16[2,32,1536]{2,1,0:T(8,128)(2,1)S(1)} custom-call(bf16[32,1536]{1,0:T(8,128)(2,1)} %tok_a.1, s32[8,32]{1,0:T(8,128)} %bitcast.26, s32[8,32]{1,0:T(8,128)} %bitcast.27, bf16[8,32]{1,0:T(8,128)(2,1)} %bitcast.32, bf16[32,1536]{1,0:T(8,128)(2,1)} %tok_b.1, s32[8,32]{1,0:T(8,128)} %bitcast.28, s32[8,32]{1,0:T(8,128)} %bitcast.29, ...), custom_call_target="tpu_custom_call" | custom-call | tf_op jit(solution)/shard_map/moe_layer/pallas_call | solution.py:505
  43.8 0.7 %slice_bitcast_fusion = (bf16[32,1536]{1,0:T(8,128)(2,1)}, bf16[32,1536]{1,0:T(8,128)(2,1)}) fusion(bf16[2,32,1536]{2,1,0:T(8,128)(2,1)S(1)} %moe_layer.1), kind=kLoop, calls=%fused_computation | loop fusion | bytes 393216 | tf_op jit(solution)/shard_map/squeeze | solution.py:520

commit v4 on v3

--- a/solution.py
+++ b/solution.py
@@ -20,7 +20,8 @@
 HALF = DIM // 2
 CHUNK = 256
 CHUNKS = DIM // CHUNK
-BLOCKS = ((0, 1), (1, 2), (2, 4), (4, 6))
+PIECES = HALF // CHUNK
+FLIPPED = (1, 2)
 ROWS = GROUP * TOKENS
 LROWS = LOCAL * GROUP * SLOTS
 F32 = jnp.float32
@@ -45,7 +46,7 @@
     out_y,
     xv, gains, ev, sv, gv,
     wqkv, wov, wgv, wuv, wdv,
-    norm_a, qkv, ctx, hv, uall, meta, disp, comb, picked, o2, part, r1, s2, r2, fin, r3,
+    wt, norm_a, qkv, ctx, hv, uall, meta, disp, comb, combt, picked, hidden, o2, part, r1, s2, r2, fin, r3,
     sem_in, sem_qkv, sem_o, sem_exp,
     msend, mrecv, dsend, drecv, osend, orecv, rsend, rrecv,
 ):
@@ -106,9 +107,12 @@
     for k in range(1, GROUP):
         pl.semaphore_signal(barrier, inc=1, device_id={"ep": flip[k]}, device_id_type=MESH)
 
-    for copy in small:
+    small[0].wait()
+    for which in range(3):
+        qkv_copy(which, 1).start()
+    for copy in small[1:]:
         copy.wait()
-    for c in range(1, CHUNKS):
+    for c in range(2, CHUNKS):
         for which in range(3):
             qkv_copy(which, c).start()
     wo_copy.start()
@@ -162,9 +166,13 @@
     def lanes(which, c):
         return qkv[which, :, c * CHUNK:(c + 1) * CHUNK]
 
-    def project(which, lo, hi):
-        cols = slice(lo * CHUNK, hi * CHUNK)
-        prod = lax.dot_general(norm_a[...], wqkv[which, cols, :], NT, preferred_element_type=F32)
+    def project(which, c):
+        cols = slice(c * CHUNK, (c + 1) * CHUNK)
+        if which in FLIPPED:
+            wt[...] = wqkv[which, cols, :].T
+            prod = jnp.dot(twice(norm_a[...]), wt[...], preferred_element_type=F32)[:n2]
+        else:
+            prod = lax.dot_general(norm_a[...], wqkv[which, cols, :], NT, preferred_element_type=F32)
         qkv[which, :, cols] = prod.astype(BF16)
 
     def scores(c):
@@ -176,35 +184,26 @@
     def store_context(c, p):
         ctx[:, c * CHUNK:(c + 1) * CHUNK] = jnp.dot(p, spread(lanes(2, c)), preferred_element_type=F32).astype(BF16)
 
-    before = ()
-    for lo, hi in BLOCKS:
-        for c in range(lo, hi):
-            for which in range(3):
-                qkv_copy(which, c).wait()
-        raw = [scores(c) for c in before]
-        project(0, lo, hi)
-        probs = [softmax(s) for s in raw]
-        project(1, lo, hi)
-        for c, p in zip(before, probs):
-            store_context(c, p)
-        project(2, lo, hi)
-        before = tuple(range(lo, hi))
-
-    def expert_copies(e):
-        return (
-            local(wg_hbm.at[e], wgv.at[e], sem_exp.at[0, e]),
-            local(wu_hbm.at[e], wuv.at[e], sem_exp.at[1, e]),
-            local(wd_hbm.at[e], wdv.at[e], sem_exp.at[2, e]),
-        )
+    for c in range(CHUNKS):
+        for which in range(3):
+            qkv_copy(which, c).wait()
+        raw = scores(c - 1) if c else None
+        project(0, c)
+        probs = softmax(raw) if c else None
+        project(1, c)
+        if c:
+            store_context(c - 1, probs)
+        project(2, c)
+
+    def expert_copy(which, e):
+        hbm, vmem = ((wg_hbm, wgv), (wu_hbm, wuv), (wd_hbm, wdv))[which]
+        return local(hbm.at[e], vmem.at[e], sem_exp.at[which, e])
 
     for e in range(LOCAL):
-        for copy in expert_copies(e):
-            copy.start()
-
-    raw = [scores(c) for c in before]
-    probs = [softmax(s) for s in raw]
-    for c, p in zip(before, probs):
-        store_context(c, p)
+        for which in range(3):
+            expert_copy(which, e).start()
+
+    store_context(CHUNKS - 1, softmax(scores(CHUNKS - 1)))
 
     wo_copy.wait()
     attn = jnp.dot(twice(ctx[...]), wov[...], preferred_element_type=F32)[:n2]
@@ -299,6 +298,9 @@
                     wide = jnp.concatenate([hit] * GROUP, axis=0)
                     disp[b, e * 64:(e + 1) * 64, :] = jnp.where(owner_hit, wide, 0.0).astype(BF16)
 
+    for b in range(2):
+        combt[b] = comb[b].T
+
     def relay(b):
         d_wait(b, 0, flip[2], 0, H)
         d_fwd_x(b).start()
@@ -327,84 +329,81 @@
             cols = slice(n * CHUNK, (n + 1) * CHUNK)
             picked[:, cols] = jnp.dot(disp[b], uall[b, :, cols], preferred_element_type=F32).astype(BF16)
 
-    def o_copy(b, e):
-        src = o2.at[b, 1 - core, pl.ds(e * 64, 64)]
-        dst = o2.at[b, 1 - core, pl.ds(LROWS + e * 64, 64)]
-        return remote(src, dst, osend.at[b, e], orecv.at[b, e], flip[1])
-
-    def o_wait(b):
+    def gate_up(b, which):
+        for e in which:
+            if b == 0:
+                expert_copy(0, e).wait()
+                expert_copy(1, e).wait()
+        for e in which:
+            x = twice(picked[e * 64:(e + 1) * 64, :])
+            g = jnp.dot(x, wgv[e], preferred_element_type=F32)[:64]
+            up = jnp.dot(x, wuv[e], preferred_element_type=F32)[:64]
+            hidden[e] = (g * (1.0 / (1.0 + jnp.exp(-g))) * up).astype(BF16)
+
+    def wait_down():
         for e in range(LOCAL):
-            ref = o2.at[b, core, pl.ds(LROWS + e * 64, 64)]
-            remote(ref, ref, osend.at[b, e], orecv.at[b, e], flip[1]).wait_recv()
-
-    def gate_up(e):
-        x = twice(picked[e * 64:(e + 1) * 64, :])
-        g = jnp.dot(x, wgv[e], preferred_element_type=F32)
-        up = jnp.dot(x, wuv[e], preferred_element_type=F32)
-        return g[:64], up[:64]
-
-    def experts(b):
-        if b == 0:
-            for e in range(LOCAL):
-                for copy in expert_copies(e):
-                    copy.wait()
-        g, up = gate_up(0)
+            expert_copy(2, e).wait()
+
+    def o_copy(b, j):
+        src = o2.at[b, 1 - core, j, pl.ds(0, LROWS)]
+        dst = o2.at[b, 1 - core, j, pl.ds(LROWS, LROWS)]
+        return remote(src, dst, osend.at[b, j], orecv.at[b, j], flip[1])
+
+    def down(b, j):
         for e in range(LOCAL):
-            hidden = (g * (1.0 / (1.0 + jnp.exp(-g))) * up).astype(BF16)
-            if e + 1 < LOCAL:
-                g, up = gate_up(e + 1)
-            o = jnp.dot(twice(hidden), wdv[e], preferred_element_type=F32)[:64].astype(BF16)
-            rows = slice(e * 64, (e + 1) * 64)
-            o2[b, 0, rows, :] = o[:, :HALF]
-            o2[b, 1, rows, :] = o[:, HALF:]
-            if e > 0:
-                o_copy(b, e - 1).start()
-        o_copy(b, LOCAL - 1).start()
-
-    def combine(b):
-        for n in range(HALF // CHUNK):
-            cols = slice(n * CHUNK, (n + 1) * CHUNK)
-            part[b, :, cols] = lax.dot_general(comb[b], o2[b, core, :, cols], TN, preferred_element_type=F32)
-
-    def chip_rows(ref, b, dev):
-        return ref.at[b, pl.ds(pl.multiple_of((dev // 2) * 64, 64), 64)]
-
-    def far_copy(b):
-        return remote(chip_rows(part, b, flip[6]), r1.at[b, 1], rsend.at[b, 0], rrecv.at[b, 0], first)
-
-    def near_copy(b):
-        return remote(chip_rows(part, b, first), r1.at[b, 0], rsend.at[b, 1], rrecv.at[b, 1], first)
-
-    def second_copy(b):
-        return remote(s2.at[b], r2.at[b], rsend.at[b, 2], rrecv.at[b, 2], second)
-
-    def last_copy(b):
-        rows = pl.ds(pl.multiple_of((1 - core) * TOKENS, TOKENS), TOKENS)
-        return remote(fin.at[b, rows], r3.at[b], rsend.at[b, 3], rrecv.at[b, 3], flip[1])
+            x = twice(hidden[e])
+            for side in range(2):
+                cols = slice(side * HALF + j * CHUNK, side * HALF + (j + 1) * CHUNK)
+                o = jnp.dot(x, wdv[e, :, cols], preferred_element_type=F32)[:64]
+                o2[b, side, j, e * 64:(e + 1) * 64, :] = o.astype(BF16)
+        o_copy(b, j).start()
 
     def wide_rows(dev):
         return pl.ds(pl.multiple_of((dev // 2) * 64, 64), 64)
 
-    def fold(b):
-        far_copy(b).wait_recv()
-        s2[b] = part[b, wide_rows(second), :] + r1[b, 1]
-        second_copy(b).start()
-
-    def finish(b):
-        near_copy(b).wait_recv()
-        second_copy(b).wait_recv()
-        fin[b] = part[b, wide_rows(me), :] + r1[b, 0] + r2[b]
-        last_copy(b).start()
-
-    def write_out(b, out):
-        last_copy(b).wait_recv()
-        mine = fin[b, pl.ds(pl.multiple_of(core * TOKENS, TOKENS), TOKENS), :]
-        other = r3[b]
-        left = jnp.where(core == 0, mine, other)
-        right = jnp.where(core == 0, other, mine)
+    def far_copy(b, j):
+        return remote(part.at[b, j, wide_rows(flip[6])], r1.at[b, 1, j], rsend.at[b, 0, j], rrecv.at[b, 0, j], first)
+
+    def near_copy(b, j):
+        return remote(part.at[b, j, wide_rows(first)], r1.at[b, 0, j], rsend.at[b, 1, j], rrecv.at[b, 1, j], first)
+
+    def second_copy(b, j):
+        return remote(s2.at[b, j], r2.at[b, j], rsend.at[b, 2, j], rrecv.at[b, 2, j], second)
+
+    def last_copy(b, j):
+        rows = pl.ds(pl.multiple_of((1 - core) * TOKENS, TOKENS), TOKENS)
+        return remote(fin.at[b, j, rows], r3.at[b, j], rsend.at[b, 3, j], rrecv.at[b, 3, j], flip[1])
+
+    def combine(b, j):
+        ref = o2.at[b, core, j, pl.ds(LROWS, LROWS)]
+        remote(ref, ref, osend.at[b, j], orecv.at[b, j], flip[1]).wait_recv()
+        part[b, j] = jnp.dot(combt[b], o2[b, core, j], preferred_element_type=F32)
+        far_copy(b, j).start()
+
+    def near_all(b):
+        for j in range(PIECES):
+            near_copy(b, j).start()
+
+    def fold(b, j):
+        far_copy(b, j).wait_recv()
+        s2[b, j] = part[b, j, wide_rows(second), :] + r1[b, 1, j]
+        second_copy(b, j).start()
+
+    def finish(b, j):
+        near_copy(b, j).wait_recv()
+        second_copy(b, j).wait_recv()
+        fin[b, j] = part[b, j, wide_rows(me), :] + r1[b, 0, j] + r2[b, j]
+        last_copy(b, j).start()
+
+    def write_out(b, j):
+        last_copy(b, j).wait_recv()
+        mine = fin[b, j, pl.ds(pl.multiple_of(core * TOKENS, TOKENS), TOKENS), :]
+        other = r3[b, j]
         rows = slice(b * TOKENS, (b + 1) * TOKENS)
-        out[:, :HALF] = (hv[rows, :HALF].astype(F32) + left).astype(BF16)
-        out[:, HALF:] = (hv[rows, HALF:].astype(F32) + right).astype(BF16)
+        for side in range(2):
+            cols = slice(side * HALF + j * CHUNK, side * HALF + (j + 1) * CHUNK)
+            mix = jnp.where(core == side, mine, other)
+            out_y[b, :, cols] = (hv[rows, cols].astype(F32) + mix).astype(BF16)
 
     relay(0)
     send_own(1)
@@ -413,26 +412,26 @@
     gathered(0)
     pick(0)
     relay(1)
+    gate_up(0, (0, 1))
     relay_near(1)
-    experts(0)
+    gate_up(0, (2, 3, 4))
+    wait_down()
+    for j in range(PIECES): down(0, j)
     relay_far(1)
-    o_wait(0)
-    combine(0)
-    far_copy(0).start()
-    near_copy(0).start()
+    for j in range(PIECES): combine(0, j)
+    near_all(0)
     gathered(1)
     pick(1)
-    experts(1)
-    fold(0)
-    o_wait(1)
-    combine(1)
-    far_copy(1).start()
-    near_copy(1).start()
-    finish(0)
-    fold(1)
-    write_out(0, out_y.at[0])
-    finish(1)
-    write_out(1, out_y.at[1])
+    gate_up(1, range(LOCAL))
+    for j in range(PIECES): fold(0, j)
+    for j in range(PIECES): down(1, j)
+    for j in range(PIECES): combine(1, j)
+    near_all(1)
+    for j in range(PIECES): finish(0, j)
+    for j in range(PIECES): fold(1, j)
+    for j in range(PIECES): write_out(0, j)
+    for j in range(PIECES): finish(1, j)
+    for j in range(PIECES): write_out(1, j)
 
     for k in range(1, GROUP):
         meta_copy(k).wait_send()
@@ -440,10 +439,11 @@
         for part_id in range(2):
             d_x(b, part_id).wait_send()
             d_y(b, part_id).wait_send()
-        for make in (d_sib, d_fwd_x, d_fwd_y, d_sib_x, d_sib_y, d_sib_d, far_copy, near_copy, second_copy, last_copy):
+        for make in (d_sib, d_fwd_x, d_fwd_y, d_sib_x, d_sib_y, d_sib_d):
             make(b).wait_send()
-        for e in range(LOCAL):
-            o_copy(b, e).wait_send()
+        for j in range(PIECES):
+            for make in (o_copy, far_copy, near_copy, second_copy, last_copy):
+                make(b, j).wait_send()
 
 
 def solution(mesh):
@@ -467,6 +467,7 @@
         VM((LOCAL, DIM, FFN), BF16),
         VM((LOCAL, DIM, FFN), BF16),
         VM((LOCAL, FFN, DIM), BF16),
+        VM((DIM, CHUNK), BF16),
         VM((2 * TOKENS, DIM), BF16),
         VM((3, 2 * TOKENS, DIM), BF16),
         VM((2 * TOKENS, DIM), BF16),
@@ -475,14 +476,16 @@
         VM((GROUP, 2, 2, SLOTS, 128), F32),
         VM((2, LROWS, ROWS), BF16),
         VM((2, 2 * LROWS, ROWS), BF16),
+        VM((2, ROWS, 2 * LROWS), BF16),
         VM((LROWS, DIM), BF16),
-        VM((2, 2, 2 * LROWS, HALF), BF16),
-        VM((2, ROWS, HALF), F32),
-        VM((2, 2, 2 * TOKENS, HALF), F32),
-        VM((2, 2 * TOKENS, HALF), F32),
-        VM((2, 2 * TOKENS, HALF), F32),
-        VM((2, 2 * TOKENS, HALF), F32),
-        VM((2, TOKENS, HALF), F32),
+        VM((LOCAL, 2 * TOKENS, FFN), BF16),
+        VM((2, 2, PIECES, 2 * LROWS, CHUNK), BF16),
+        VM((2, PIECES, ROWS, CHUNK), F32),
+        VM((2, 2, PIECES, 2 * TOKENS, CHUNK), F32),
+        VM((2, PIECES, 2 * TOKENS, CHUNK), F32),
+        VM((2, PIECES, 2 * TOKENS, CHUNK), F32),
+        VM((2, PIECES, 2 * TOKENS, CHUNK), F32),
+        VM((2, PIECES, TOKENS, CHUNK), F32),
         DMA((10,)),
         DMA((3, CHUNKS)),
         DMA,
@@ -491,10 +494,10 @@
         DMA((GROUP,)),
         DMA((2, 10)),
         DMA((2, 10)),
-        DMA((2, LOCAL)),
-        DMA((2, LOCAL)),
-        DMA((2, 4)),
-        DMA((2, 4)),
+        DMA((2, PIECES)),
+        DMA((2, PIECES)),
+        DMA((2, 4, PIECES)),
+        DMA((2, 4, PIECES)),
     ]
 
     def device_fn(tokens_a, experts_a, slots_a, gates_a, tokens_b, experts_b, slots_b, gates_b, attn_gain, w_query, w_key, w_value, w_out, moe_gain, w_gate, w_up, w_down):

time: 44.6 us -> 42.1 us (0.944)
  Pallas kernels: 43.2 us -> 40.6 us
    pallas_call x1, Pallas kernels: 43.2 us -> 40.6 us  [device_fn(): pl.pallas_call(kernel, out_shape=out, in_specs=[hbm_spec] * 17, out_specs...]
where the time goes in v4:
time: 42.1 us; the launch traced here: 42 us
  Pallas kernels  40.6 us (96%)
  local copies, waits for them, and re-layouts  0.69 us (2%)
  between operations  0.65 us (2%)
    pallas_call x1, Pallas kernels, device_fn(): pl.pallas_call(kernel, out_shape=out, in_specs=[hbm_spec] * 17, out_specs...  40.6 us

profile of v4, /device:TPU:0, one launch (start us, length us, event | category | flops | bytes accessed | tf_op | source)
XLA Modules:
  0.0 42.0 jit_solution(17886786265514499517)
XLA Ops:
  0.6 40.6 %moe_layer.1 = bf16[2,32,1536]{2,1,0:T(8,128)(2,1)S(1)} custom-call(bf16[32,1536]{1,0:T(8,128)(2,1)} %tok_a.1, s32[8,32]{1,0:T(8,128)} %bitcast.26, s32[8,32]{1,0:T(8,128)} %bitcast.27, bf16[8,32]{1,0:T(8,128)(2,1)} %bitcast.32, bf16[32,1536]{1,0:T(8,128)(2,1)} %tok_b.1, s32[8,32]{1,0:T(8,128)} %bitcast.28, s32[8,32]{1,0:T(8,128)} %bitcast.29, ...), custom_call_target="tpu_custom_call" | custom-call | tf_op jit(solution)/shard_map/moe_layer/pallas_call | solution.py:508
  41.3 0.7 %slice_bitcast_fusion = (bf16[32,1536]{1,0:T(8,128)(2,1)}, bf16[32,1536]{1,0:T(8,128)(2,1)}) fusion(bf16[2,32,1536]{2,1,0:T(8,128)(2,1)S(1)} %moe_layer.1), kind=kLoop, calls=%fused_computation | loop fusion | bytes 393216 | tf_op jit(solution)/shard_map/squeeze | solution.py:523
